TPU v7x, 32 devices: a whole 2x2x4 slice. The times are simulated.
32 devices in a mesh: rep: 2 (over x), data: 4 (over z), expert: 4 (over y, core).
Axes of the slice: x: 2, y: 2, z: 4, core: 2. Of those that a mesh axis runs over, the one named last changes fastest.
Arguments:
- x: bfloat16 [131072, 768], P(('rep', 'expert', 'data')), parts along dimension 0
- expert_idx: int32 [131072, 1], P(('rep', 'expert', 'data')), parts along dimension 0
- gate: float32 [131072, 1], P(('rep', 'expert', 'data')), parts along dimension 0
- w_gate: bfloat16 [8, 768, 3072], P('expert', 'data')
- w_up: bfloat16 [8, 768, 3072], P('expert', 'data')
- w_down: bfloat16 [8, 3072, 768], P('expert', None, 'data')
Outputs:
- output: bfloat16 [131072, 768], P(('rep', 'expert', 'data')), parts along dimension 0
There are 2 independent parts. A program takes and returns all parts, laid end to end along the dimension named above; an argument that names none is the same for every part.
All inputs are finite; a program needn't handle non-finite values.
Results may differ from a plain program's by a relative error of at most 0.001.
Values are sent between devices in bfloat16 or wider.
A program may use at most 1 GiB of HBM per device.

v0:
```python
import jax
import jax.numpy as jnp
from jax import lax
from jax.sharding import PartitionSpec as P


def capacity_rows(tok_rows, top_k, n_exp):
    return max(8, ((5 * top_k * tok_rows) // (4 * n_exp) + 7) // 8 * 8)


def slot_table(ids_flat, n_exp, n_group, capacity):
    n_local = n_exp // n_group
    one_hot = (ids_flat[:, None] == jnp.arange(n_exp, dtype=jnp.int32)[None, :]).astype(jnp.int32)
    slot_ids = jnp.sum((jnp.cumsum(one_hot, axis=0) - one_hot) * one_hot, axis=1)
    row_base = (ids_flat % n_local) * (n_group * capacity) + (ids_flat // n_local) * capacity
    return jnp.where(slot_ids < capacity, row_base + slot_ids, n_exp * capacity)


def dispatch_rows(x_loc, dest_row, n_slots, top_k):
    tok_rows = x_loc.shape[0]
    pair_token = jnp.arange(dest_row.shape[0], dtype=jnp.int32) // top_k
    src_tok = jnp.full((n_slots,), tok_rows, jnp.int32).at[dest_row].set(pair_token, mode="drop")
    return jnp.take(x_loc, src_tok, axis=0, mode="fill", fill_value=0)


def combine_rows(x_loc, gate_loc, back_rows, dest_row):
    tok_rows, d_model = x_loc.shape
    pair_out = jnp.take(back_rows, dest_row, axis=0, mode="fill", fill_value=0)
    mixed = jnp.sum(pair_out.reshape(tok_rows, gate_loc.shape[1], d_model) * gate_loc[:, :, None], axis=1)
    return (x_loc.astype(jnp.float32) + mixed).astype(jnp.bfloat16)


def expert_ffn(expert_rows, w_gate, w_up, w_down):
    gate_act = jnp.einsum("erd,edf->erf", expert_rows, w_gate, preferred_element_type=jnp.float32)
    up_act = jnp.einsum("erd,edf->erf", expert_rows, w_up, preferred_element_type=jnp.float32)
    hidden = (jax.nn.silu(gate_act) * up_act).astype(jnp.bfloat16)
    return jnp.einsum("erf,efd->erd", hidden, w_down, preferred_element_type=jnp.float32).astype(jnp.bfloat16)


def solution(mesh):
    n_group = mesh.shape["expert"]
    tok_spec = P(("rep", "expert", "data"), None)
    wide_spec = P("expert", "data", None)
    down_spec = P("expert", None, "data")

    def device_step(x_loc, idx_loc, gate_loc, wg_loc, wu_loc, wd_loc):
        tok_rows, d_model = x_loc.shape
        top_k = idx_loc.shape[1]
        n_local = wg_loc.shape[0]
        n_exp = n_local * n_group
        capacity = capacity_rows(tok_rows, top_k, n_exp)
        dest_row = slot_table(idx_loc.reshape(tok_rows * top_k), n_exp, n_group, capacity)
        send_rows = dispatch_rows(x_loc, dest_row, n_exp * capacity, top_k).reshape(n_local, n_group, capacity, d_model)
        recv_rows = lax.all_to_all(send_rows, "expert", 1, 1, tiled=True)
        wg_full = lax.all_gather(wg_loc, "data", axis=1, tiled=True)
        wu_full = lax.all_gather(wu_loc, "data", axis=1, tiled=True)
        wd_full = lax.all_gather(wd_loc, "data", axis=2, tiled=True)
        out_rows = expert_ffn(recv_rows.reshape(n_local, n_group * capacity, d_model), wg_full, wu_full, wd_full)
        back_rows = lax.all_to_all(out_rows.reshape(n_local, n_group, capacity, d_model), "expert", 1, 1, tiled=True)
        return combine_rows(x_loc, gate_loc, back_rows.reshape(n_exp * capacity, d_model), dest_row)

    return jax.shard_map(device_step, mesh=mesh, in_specs=(tok_spec, tok_spec, tok_spec, wide_spec, wide_spec, down_spec), out_specs=tok_spec, check_vma=False)
```

profile of v0, /device:TPU:0, one launch (start us, length us, event | category | flops | bytes accessed | tf_op | source)
XLA Modules:
  0.0 685.6 jit_solution(10877761120273491090)
XLA Ops:
  6.5 0.0 all-gather.4.cloned.1.call-start
  6.5 0.7 all-gather.4.cloned.1.call-update
  7.3 0.0 all-gather.6.cloned.1.call-start
  7.3 0.7 all-gather.6.cloned.1.call-update
  8.0 0.7 fusion.5
  8.7 2.3 reduce-window.6
  11.1 0.3 slice_reduce_fusion
  11.4 0.2 reduce-window.9
  11.5 0.1 add_bitcast_fusion
  11.7 0.8 fusion.4
  12.5 1.5 and_reduce_fusion
  14.0 0.0 copy-start
  14.0 15.5 %scatter_custom_fusion = s32[5120]{0:T(1024)S(1)} fusion(s32[4096]{0:T(1024)S(1)} %bitcast.49, s32[4096]{0:T(1024)S(1)} %iota.11, s32[]{:T(128)} %constant.77.clone.1), kind=kCustom, calls=%fused_computation.31 | custom fusion | bytes 20484 | tf_op jit(solution)/shard_map/scatter | solution.py:22
  29.6 0.0 copy-done
  29.6 27.2 %gather_fusion = bf16[5120,768]{1,0:T(8,128)(2,1)} fusion(bf16[4096,768]{1,0:T(8,128)(2,1)} %param.6, s32[5120]{0:T(1024)S(1)} %fusion.6), kind=kCustom, calls=%fused_computation | custom fusion | bytes 15749120 | tf_op jit(solution)/shard_map/jit(_take)/gather | solution.py:23
  56.8 7.0 %copy_select_fusion = bf16[2,4,640,768]{3,2,0,1:T(8,128)(2,1)} fusion(bf16[2,4,640,768]{3,2,1,0:T(8,128)(2,1)} %bitcast.42, pred[2,4,640]{2,0,1:T(4,128)(4,1)S(1)} %copy.11), kind=kLoop, calls=%fused_computation.6 | loop fusion | flops 3932160 | bytes 15733760 | tf_op jit(solution)/shard_map/jit(_take)/select_n | solution.py:23
  63.8 5.6 all-to-all-start
  69.4 0.2 all-gather.8.cloned.1.call-start
  69.6 0.5 all-gather.8.cloned.1.call-update
  70.1 87.2 %all-to-all-done = bf16[2,4,640,768]{3,2,0,1:T(8,128)(2,1)} async-done(((bf16[2,4,640,768]{3,2,0,1:T(8,128)(2,1)}), bf16[2,4,640,768]{3,2,0,1:T(8,128)(2,1)}, u32[]{:S(2)}, u32[]{:S(2)}) %all-to-all-start) | async-done | bytes 7864352 | tf_op jit(solution)/shard_map/all_to_all | solution.py:54
  157.4 6.8 copy.13
  164.2 14.3 %all-gather.4.cloned.1.call-done = bf16[2,768,3072]{2,1,0:T(8,128)(2,1)} async-done(((bf16[2,192,3072]{2,1,0:T(8,128)(2,1)}), bf16[2,768,3072]{2,1,0:T(8,128)(2,1)}) %all-gather.4.cloned.1.call-update) | async-done | bytes 9437200 | tf_op jit(solution)/shard_map/all_gather | solution.py:55
  178.5 36.5 %fusion.13 = f32[2,2560,3072]{2,1,0:T(8,128)} fusion(bf16[2,2560,768]{2,1,0:T(8,128)(2,1)} %bitcast.43, bf16[2,768,3072]{2,1,0:T(8,128)(2,1)} %all-gather.4.cloned.1.call-done), kind=kOutput, calls=%fused_computation.35 | convolution fusion | flops 24159191040 | bytes 80216064 | tf_op jit(solution)/shard_map/erd,edf->erf/dot_general | solution.py:34
  215.0 130.3 %all-gather.6.cloned.1.call-done = bf16[2,768,3072]{2,1,0:T(8,128)(2,1)} async-done(((bf16[2,192,3072]{2,1,0:T(8,128)(2,1)}), bf16[2,768,3072]{2,1,0:T(8,128)(2,1)}) %all-gather.6.cloned.1.call-update) | async-done | bytes 9437200 | tf_op jit(solution)/shard_map/all_gather | solution.py:56
  345.3 43.8 %multiply_convert_fusion.clone.6 = bf16[2,2560,3072]{2,1,0:T(8,128)(2,1)} fusion(f32[2,2560,3072]{2,1,0:T(8,128)} %fusion.13, bf16[2,2560,768]{2,1,0:T(8,128)(2,1)} %bitcast.44, bf16[2,768,3072]{2,1,0:T(8,128)(2,1)} %all-gather.6.cloned.1.call-done), kind=kOutput, calls=%fused_computation.3.clone.clone.clone.clone.clone.1 | convolution fusion | flops 24253562880 | bytes 111673344 | tf_op jit(solution)/shard_map/erd,edf->erf/dot_general | solution.py:35
  389.1 122.9 %all-gather.8.cloned.1.call-done = bf16[2,3072,768]{1,2,0:T(8,128)(2,1)} async-done(((bf16[2,3072,192]{1,2,0:T(8,128)(2,1)}), bf16[2,3072,768]{1,2,0:T(8,128)(2,1)}) %all-gather.8.cloned.1.call-update) | async-done | bytes 9437200 | tf_op jit(solution)/shard_map/all_gather | solution.py:57
  512.0 30.9 %fusion.1 = bf16[2,2560,768]{2,1,0:T(8,128)(2,1)S(1)} fusion(bf16[2,3072,768]{1,2,0:T(8,128)(2,1)} %all-gather.8.cloned.1.call-done, bf16[2,2560,3072]{2,1,0:T(8,128)(2,1)} %multiply_convert_fusion.clone.6), kind=kOutput, calls=%fused_computation.7 | convolution fusion | flops 24163123200 | bytes 48758784 | tf_op jit(solution)/shard_map/erf,efd->erd/dot_general | solution.py:37
  543.0 3.7 copy.14
  546.7 0.0 copy-start.1
  546.7 5.7 all-to-all-start.1
  552.4 0.0 copy-done.1
  552.4 87.2 %all-to-all-done.1 = bf16[2,4,640,768]{3,2,0,1:T(8,128)(2,1)} async-done(((bf16[2,4,640,768]{3,2,0,1:T(8,128)(2,1)}), bf16[2,4,640,768]{3,2,0,1:T(8,128)(2,1)}, u32[]{:S(2)}, u32[]{:S(2)}) %all-to-all-start.1) | async-done | bytes 7864352 | tf_op jit(solution)/shard_map/all_to_all | solution.py:59
  639.6 6.9 %copy.15 = bf16[2,4,640,768]{3,2,1,0:T(8,128)(2,1)} copy(bf16[2,4,640,768]{3,2,0,1:T(8,128)(2,1)} %all-to-all-done.1) | data formatting | bytes 15728640 | tf_op jit(solution)/shard_map/all_to_all | solution.py:59
  646.5 0.0 copy-start.2
  646.5 0.0 copy-start.3
  646.5 23.3 %gather_fusion.1 = bf16[4096,768]{1,0:T(8,128)(2,1)} fusion(bf16[5120,768]{1,0:T(8,128)(2,1)} %bitcast.41, s32[4096]{0:T(1024)S(1)} %broadcast_clamp_fusion), kind=kCustom, calls=%fused_computation.1 | custom fusion | bytes 12599296 | tf_op jit(solution)/shard_map/jit(_take)/gather | solution.py:28
  669.8 0.0 copy-done.2
  669.8 0.0 copy-done.3
  669.8 9.3 %add_convert_fusion = bf16[4096,768]{1,0:T(8,128)(2,1)} fusion(bf16[4096,768]{1,0:T(8,128)(2,1)} %param.6, f32[4096]{0:T(1024)S(1)} %bitcast.52, bf16[4096,768]{1,0:T(8,128)(2,1)} %gather_fusion.1, pred[4096]{0:T(1024)(128)(4,1)S(1)} %copy-done.2), kind=kLoop, calls=%fused_computation.5 | loop fusion | flops 18874368 | bytes 18894848 | tf_op jit(solution)/shard_map/convert_element_type | solution.py:30
  (6 shorter events, 0.1 us)
Async XLA Ops:
  6.5 172.0 %all-gather.4.cloned.1.call-start = ((), (), s32[]{:S(2)}) async-start(), calls=%async_computation.2 | async-start | bytes 11796480 | tf_op jit(solution)/shard_map/all_gather | solution.py:55
  7.3 338.0 %all-gather.6.cloned.1.call-start = ((), (), s32[]{:S(2)}) async-start(), calls=%async_computation.3 | async-start | bytes 11796480 | tf_op jit(solution)/shard_map/all_gather | solution.py:56
  14.0 15.6 %copy-start = (s32[4096,1]{0,1:T(1,128)}, s32[4096,1]{0,1:T(1,128)S(1)}, u32[]{:S(2)}) copy-start(s32[4096,1]{0,1:T(1,128)S(1)} %get-tuple-element.6) | copy-start | bytes 49156
  63.8 93.5 %all-to-all-start = ((bf16[2,4,640,768]{3,2,0,1:T(8,128)(2,1)}), bf16[2,4,640,768]{3,2,0,1:T(8,128)(2,1)}, u32[]{:S(2)}, u32[]{:S(2)}) async-start(bf16[2,4,640,768]{3,2,0,1:T(8,128)(2,1)} %copy_select_fusion), calls=%async_computation | async-start | bytes 15728640 | tf_op jit(solution)/shard_map/all_to_all | solution.py:54
  69.4 442.6 %all-gather.8.cloned.1.call-start = ((), (), s32[]{:S(2)}) async-start(), calls=%async_computation.4 | async-start | bytes 11796480 | tf_op jit(solution)/shard_map/all_gather | solution.py:57
  546.7 5.7 copy-start.1
  546.7 92.9 %all-to-all-start.1 = ((bf16[2,4,640,768]{3,2,0,1:T(8,128)(2,1)}), bf16[2,4,640,768]{3,2,0,1:T(8,128)(2,1)}, u32[]{:S(2)}, u32[]{:S(2)}) async-start(bf16[2,4,640,768]{3,2,0,1:T(8,128)(2,1)} %copy.14), calls=%async_computation.1 | async-start | bytes 15728640 | tf_op jit(solution)/shard_map/all_to_all | solution.py:59
  646.5 23.3 %copy-start.2 = (pred[4096]{0:T(1024)(128)(4,1)S(1)}, pred[4096]{0:T(1024)(128)(4,1)}, u32[]{:S(2)}) copy-start(pred[4096]{0:T(1024)(128)(4,1)} %get-tuple-element.5) | copy-start | bytes 12292
  646.5 23.3 %copy-start.3 = (f32[4096,1]{0,1:T(1,128)S(1)}, f32[4096,1]{0,1:T(1,128)}, u32[]{:S(2)}) copy-start(f32[4096,1]{0,1:T(1,128)} %param.8) | copy-start | bytes 49156
Sparse Core Ops, SparseCore 0:
  8.9 169.5 all-gather.3
  180.1 165.1 all-gather.5
  346.8 165.1 all-gather.7
where the time goes:
time: 686 us
  waiting for transfers between devices  444 us (65%)
  matrix products  111 us (16%)
  local copies, waits for them, and re-layouts  83.8 us (12%)
  other arithmetic  22 us (3%)
  between operations  13.2 us (2%)
  starting transfers between devices  11.5 us (2%)
    all_gather x1, waiting for transfers between devices, device_step(): wu_full = lax.all_gather(wu_loc, 'data', axis=1, tiled=True)  130 us
    all_gather x1, waiting for transfers between devices, device_step(): wd_full = lax.all_gather(wd_loc, 'data', axis=2, tiled=True)  123 us
    all_to_all x1, waiting for transfers between devices, device_step(): recv_rows = lax.all_to_all(send_rows, 'expert', 1, 1, tiled=True)  87.2 us
    all_to_all x1, waiting for transfers between devices, device_step(): lax.all_to_all(out_rows.reshape(n_local, n_group, capacity, d_model), 'ex...  87.2 us
    dot_general x1, matrix products, expert_ffn(): jnp.einsum('erd,edf->erf', expert_rows, w_up, preferred_element_type=jnp....  43.8 us
    dot_general x1, matrix products, expert_ffn(): jnp.einsum('erd,edf->erf', expert_rows, w_gate, preferred_element_type=jn...  36.5 us
    dot_general x1, matrix products, expert_ffn(): jnp.einsum('erf,efd->erd', hidden, w_down, preferred_element_type=jnp.flo...  30.9 us
    gather x1, local copies, waits for them, and re-layouts, dispatch_rows(): return jnp.take(x_loc, src_tok, axis=0, mode='fill', fill_value=0)  27.2 us
  transfers between devices with their start and end apart: 5, of which 5 were waited for; matrix products, arithmetic and copies ran while one was open for 21% of the time, Pallas kernels for 0%

commit v1 on v0

v1 whole, which is shorter than its diff:
```python
import jax
import jax.numpy as jnp
from jax import lax
from jax.sharding import PartitionSpec as P


def capacity_rows(tok_rows, top_k, n_exp):
    return max(8, ((5 * top_k * tok_rows) // (4 * n_exp) + 7) // 8 * 8)


def slot_table(ids_flat, n_exp, capacity):
    one_hot = (ids_flat[:, None] == jnp.arange(n_exp, dtype=jnp.int32)[None, :]).astype(jnp.int32)
    slot_ids = jnp.sum((jnp.cumsum(one_hot, axis=0) - one_hot) * one_hot, axis=1)
    return jnp.where(slot_ids < capacity, ids_flat * capacity + slot_ids, n_exp * capacity)


def dispatch_rows(x_loc, dest_row, n_slots, top_k):
    tok_rows = x_loc.shape[0]
    pair_token = jnp.arange(dest_row.shape[0], dtype=jnp.int32) // top_k
    src_tok = jnp.full((n_slots,), tok_rows, jnp.int32).at[dest_row].set(pair_token, mode="drop")
    return jnp.take(x_loc, src_tok, axis=0, mode="fill", fill_value=0)


def combine_rows(x_loc, gate_loc, back_rows, dest_row):
    tok_rows, d_model = x_loc.shape
    pair_out = jnp.take(back_rows, dest_row, axis=0, mode="fill", fill_value=0)
    mixed = jnp.sum(pair_out.reshape(tok_rows, gate_loc.shape[1], d_model) * gate_loc[:, :, None], axis=1)
    return (x_loc.astype(jnp.float32) + mixed).astype(jnp.bfloat16)


def expert_ffn(expert_rows, w_gate, w_up, w_down):
    gate_act = jnp.dot(expert_rows, w_gate, preferred_element_type=jnp.float32)
    up_act = jnp.dot(expert_rows, w_up, preferred_element_type=jnp.float32)
    hidden = (jax.nn.silu(gate_act) * up_act).astype(jnp.bfloat16)
    return jnp.dot(hidden, w_down, preferred_element_type=jnp.float32).astype(jnp.bfloat16)


def solution(mesh):
    n_rep, n_group = mesh.shape["rep"], mesh.shape["expert"]
    tok_spec = P(("rep", "expert", "data"), None)
    wide_spec = P("expert", "data", None)
    down_spec = P("expert", None, "data")

    def device_step(x_loc, idx_loc, gate_loc, wg_loc, wu_loc, wd_loc):
        tok_rows, d_model = x_loc.shape
        top_k = idx_loc.shape[1]
        n_exp = wg_loc.shape[0] * n_group
        capacity = capacity_rows(tok_rows, top_k, n_exp)
        mine = lax.axis_index("rep")
        wg_full = lax.all_gather(lax.dynamic_index_in_dim(wg_loc, mine, 0, False), "data", axis=0, tiled=True)
        wu_full = lax.all_gather(lax.dynamic_index_in_dim(wu_loc, mine, 0, False), "data", axis=0, tiled=True)
        wd_full = lax.all_gather(lax.dynamic_index_in_dim(wd_loc, mine, 0, False), "data", axis=1, tiled=True)
        dest_row = slot_table(idx_loc.reshape(tok_rows * top_k), n_exp, capacity)
        send_rows = dispatch_rows(x_loc, dest_row, n_exp * capacity, top_k).reshape(n_exp, capacity, d_model)
        recv_rows = lax.all_to_all(send_rows, ("expert", "rep"), 0, 0, tiled=True)
        out_rows = expert_ffn(recv_rows.reshape(n_exp * capacity, d_model), wg_full, wu_full, wd_full)
        back_rows = lax.all_to_all(out_rows.reshape(n_exp, capacity, d_model), ("expert", "rep"), 0, 0, tiled=True)
        return combine_rows(x_loc, gate_loc, back_rows.reshape(n_exp * capacity, d_model), dest_row)

    return jax.shard_map(device_step, mesh=mesh, in_specs=(tok_spec, tok_spec, tok_spec, wide_spec, wide_spec, down_spec), out_specs=tok_spec, check_vma=False)
```

time: 686 us -> 443 us (0.65)
  waiting for transfers between devices: 444 us -> 214 us
  local copies, waits for them, and re-layouts: 83.8 us -> 73.3 us
    all_gather x3, waiting for transfers between devices: 268 us -> 40.2 us  [the longest x1 40.2 us: device_step(): lax.all_gather(lax.dynamic_index_in_dim(wd_loc, mine, 0, False), 'data',...]
    all_to_all x2 -> x0, local copies, waits for them, and re-layouts: 13.7 us -> none  [the longest x1 6.91 us: device_step(): lax.all_to_all(out_rows.reshape(n_local, n_group, capacity, d_model), 'ex...]
  transfers between devices with their start and end apart: 5 -> 5, of which waited for: 5 -> 3; matrix products, arithmetic and copies ran while one was open for 21% -> 31% of each run, Pallas kernels for 0% -> 0%
where the time goes in v1:
time: 443 us; the launch traced here: 442 us
  waiting for transfers between devices  214 us (48%)
  matrix products  110 us (25%)
  local copies, waits for them, and re-layouts  73.3 us (17%)
  other arithmetic  20.7 us (5%)
  between operations  13.2 us (3%)
  starting transfers between devices  10.8 us (2%)
    all_to_all x1, waiting for transfers between devices, device_step(): lax.all_to_all(out_rows.reshape(n_exp, capacity, d_model), ('expert', 're...  87.6 us
    all_to_all x1, waiting for transfers between devices, device_step(): recv_rows = lax.all_to_all(send_rows, ('expert', 'rep'), 0, 0, tiled=True)  86.3 us
    dot_general x1, matrix products, expert_ffn(): up_act = jnp.dot(expert_rows, w_up, preferred_element_type=jnp.float32)  44.1 us
    all_gather x1, waiting for transfers between devices, device_step(): lax.all_gather(lax.dynamic_index_in_dim(wd_loc, mine, 0, False), 'data',...  40.2 us
    dot_general x1, matrix products, expert_ffn(): gate_act = jnp.dot(expert_rows, w_gate, preferred_element_type=jnp.float32)  35.2 us
    dot_general x1, matrix products, expert_ffn(): jnp.dot(hidden, w_down, preferred_element_type=jnp.float32)  30.7 us
    gather x1, local copies, waits for them, and re-layouts, dispatch_rows(): return jnp.take(x_loc, src_tok, axis=0, mode='fill', fill_value=0)  27.2 us
    gather x1, local copies, waits for them, and re-layouts, combine_rows(): pair_out = jnp.take(back_rows, dest_row, axis=0, mode='fill', fill_value=0)  23.3 us
  transfers between devices with their start and end apart: 5, of which 3 were waited for; matrix products, arithmetic and copies ran while one was open for 31% of the time, Pallas kernels for 0%

profile of v1, /device:TPU:0, one launch (start us, length us, event | category | flops | bytes accessed | tf_op | source)
XLA Modules:
  0.0 442.1 jit_solution(1894127563676601578)
XLA Ops:
  6.5 0.0 copy-start
  6.5 0.0 copy-start.3
  6.5 0.0 all-gather.7.cloned.1.call-start
  6.5 1.7 copy-done
  8.2 1.1 constant_dynamic-slice_fusion.2
  9.3 0.0 all-gather.7.cloned.1.call-update
  9.3 0.0 all-gather.9.cloned.1.call-start
  9.4 2.4 constant_dynamic-slice_fusion.1
  11.8 0.0 all-gather.9.cloned.1.call-update
  11.8 0.7 fusion.10
  12.6 2.3 reduce-window.6
  14.9 0.3 slice_reduce_fusion
  15.2 0.2 reduce-window.9
  15.4 0.1 add_bitcast_fusion
  15.5 0.0 copy-done.3
  15.5 0.1 fusion.9
  15.6 0.7 and_reduce_fusion
  16.3 0.0 copy-start.4
  16.3 0.6 copy-done.4
  16.9 15.5 %scatter_custom_fusion = s32[5120]{0:T(1024)S(1)} fusion(s32[4096]{0:T(1024)S(1)} %bitcast.53, s32[4096]{0:T(1024)S(1)} %iota.11, s32[]{:T(128)} %constant.66.clone.1), kind=kCustom, calls=%fused_computation.27 | custom fusion | bytes 20484 | tf_op jit(solution)/shard_map/scatter | solution.py:20
  32.5 27.2 %gather_fusion = bf16[5120,768]{1,0:T(8,128)(2,1)} fusion(bf16[4096,768]{1,0:T(8,128)(2,1)} %param.6, s32[5120]{0:T(1024)S(1)} %fusion.11), kind=kCustom, calls=%fused_computation | custom fusion | bytes 15749120 | tf_op jit(solution)/shard_map/jit(_take)/gather | solution.py:21
  59.8 7.1 %broadcast_select_fusion = bf16[8,640,768]{2,1,0:T(8,128)(2,1)} fusion(bf16[8,640,768]{2,1,0:T(8,128)(2,1)} %bitcast.48, pred[8,640]{1,0:T(8,128)(4,1)S(1)} %broadcast_in_dim.40), kind=kLoop, calls=%fused_computation.7 | loop fusion | flops 3932160 | bytes 15733760 | tf_op jit(solution)/shard_map/jit(_take)/select_n | solution.py:21
  66.9 0.0 copy-start.2
  66.9 5.4 %all-to-all-start = ((bf16[8,640,768]{2,1,0:T(8,128)(2,1)}), bf16[8,640,768]{2,1,0:T(8,128)(2,1)}, u32[]{:S(2)}, u32[]{:S(2)}) async-start(bf16[8,640,768]{2,1,0:T(8,128)(2,1)} %broadcast_select_fusion), calls=%async_computation | async-start | bytes 15728640 | tf_op jit(solution)/shard_map/all_to_all | solution.py:55
  72.2 0.2 all-gather.11.cloned.1.call-start
  72.5 0.0 copy-done.2
  72.5 1.1 constant_dynamic-slice_fusion
  73.6 0.0 all-gather.11.cloned.1.call-update
  73.6 86.3 %all-to-all-done = bf16[8,640,768]{2,1,0:T(8,128)(2,1)} async-done(((bf16[8,640,768]{2,1,0:T(8,128)(2,1)}), bf16[8,640,768]{2,1,0:T(8,128)(2,1)}, u32[]{:S(2)}, u32[]{:S(2)}) %all-to-all-start) | async-done | bytes 7864352 | tf_op jit(solution)/shard_map/all_to_all | solution.py:55
  159.9 0.0 all-gather.7.cloned.1.call-done
  159.9 35.2 %fusion.5 = f32[5120,3072]{1,0:T(8,128)} fusion(bf16[5120,768]{1,0:T(8,128)(2,1)} %bitcast.6, bf16[1,768,3072]{2,1,0:T(8,128)(2,1)} %all-gather.7.cloned.1.call-done), kind=kOutput, calls=%fused_computation.10 | convolution fusion | flops 24159191040 | bytes 75497472 | tf_op jit(solution)/shard_map/dot_general | solution.py:32
  195.1 0.0 all-gather.9.cloned.1.call-done
  195.1 44.1 %multiply_convert_fusion.clone.6 = bf16[5120,3072]{1,0:T(8,128)(2,1)} fusion(f32[5120,3072]{1,0:T(8,128)} %fusion.5, bf16[5120,768]{1,0:T(8,128)(2,1)} %bitcast.6, bf16[1,768,3072]{2,1,0:T(8,128)(2,1)} %all-gather.9.cloned.1.call-done), kind=kOutput, calls=%fused_computation.3.clone.clone.clone.clone.clone.1 | convolution fusion | flops 24253562880 | bytes 106954752 | tf_op jit(solution)/shard_map/dot_general | solution.py:33
  239.2 40.2 %all-gather.11.cloned.1.call-done = bf16[1,3072,768]{1,2,0:T(8,128)(2,1)} async-done(((bf16[1,3072,192]{1,2,0:T(8,128)(2,1)}), bf16[1,3072,768]{1,2,0:T(8,128)(2,1)}) %all-gather.11.cloned.1.call-update) | async-done | bytes 4718608 | tf_op jit(solution)/shard_map/all_gather | solution.py:52
  279.3 30.7 %fusion.1 = bf16[5120,768]{1,0:T(8,128)(2,1)} fusion(bf16[1,3072,768]{1,2,0:T(8,128)(2,1)} %all-gather.11.cloned.1.call-done, bf16[5120,3072]{1,0:T(8,128)(2,1)} %multiply_convert_fusion.clone.6), kind=kOutput, calls=%fused_computation.6 | convolution fusion | flops 24163123200 | bytes 44040192 | tf_op jit(solution)/shard_map/dot_general | solution.py:35
  310.0 0.0 copy-start.5
  310.0 5.1 %all-to-all-start.1 = ((bf16[8,640,768]{2,1,0:T(8,128)(2,1)}), bf16[8,640,768]{2,1,0:T(8,128)(2,1)}, u32[]{:S(2)}, u32[]{:S(2)}) async-start(bf16[8,640,768]{2,1,0:T(8,128)(2,1)} %bitcast.49), calls=%async_computation.1 | async-start | bytes 15728640 | tf_op jit(solution)/shard_map/all_to_all | solution.py:57
  315.2 0.0 copy-done.5
  315.2 87.6 %all-to-all-done.1 = bf16[8,640,768]{2,1,0:T(8,128)(2,1)} async-done(((bf16[8,640,768]{2,1,0:T(8,128)(2,1)}), bf16[8,640,768]{2,1,0:T(8,128)(2,1)}, u32[]{:S(2)}, u32[]{:S(2)}) %all-to-all-start.1) | async-done | bytes 7864352 | tf_op jit(solution)/shard_map/all_to_all | solution.py:57
  402.7 0.0 copy-start.6
  402.7 0.0 copy-start.7
  402.8 23.3 %gather_fusion.1 = bf16[4096,768]{1,0:T(8,128)(2,1)} fusion(bf16[5120,768]{1,0:T(8,128)(2,1)} %bitcast.11, s32[4096]{0:T(1024)S(1)} %broadcast_clamp_fusion), kind=kCustom, calls=%fused_computation.1 | custom fusion | bytes 12599296 | tf_op jit(solution)/shard_map/jit(_take)/gather | solution.py:26
  426.1 0.0 copy-start.1
  426.1 0.0 copy-done.6
  426.1 0.0 copy-done.7
  426.1 9.5 %add_convert_fusion = bf16[4096,768]{1,0:T(8,128)(2,1)} fusion(bf16[4096,768]{1,0:T(8,128)(2,1)} %param.6, f32[4096]{0:T(1024)S(1)} %bitcast.56, bf16[4096,768]{1,0:T(8,128)(2,1)} %gather_fusion.1, pred[4096]{0:T(1024)(128)(4,1)S(1)} %copy-done.6), kind=kLoop, calls=%fused_computation.4 | loop fusion | flops 18874368 | bytes 18894848 | tf_op jit(solution)/shard_map/convert_element_type | solution.py:28
  435.5 0.0 copy-done.1
  (5 shorter events, 0.1 us)
Async XLA Ops:
  6.5 1.7 copy-start
  6.5 8.9 %copy-start.3 = (s32[4096,1]{0,1:T(1,128)S(1)}, s32[4096,1]{0,1:T(1,128)}, u32[]{:S(2)}) copy-start(s32[4096,1]{0,1:T(1,128)} %param.7) | copy-start | bytes 49156
  6.5 153.4 %all-gather.7.cloned.1.call-start = ((), (), s32[]{:S(2)}) async-start(), calls=%async_computation.2 | async-start | bytes 5898240 | tf_op jit(solution)/shard_map/all_gather | solution.py:50
  9.3 185.8 %all-gather.9.cloned.1.call-start = ((), (), s32[]{:S(2)}) async-start(), calls=%async_computation.3 | async-start | bytes 5898240 | tf_op jit(solution)/shard_map/all_gather | solution.py:51
  16.3 0.6 copy-start.4
  66.9 5.6 %copy-start.2 = (bf16[2,3072,192]{1,2,0:T(8,128)(2,1)S(1)}, bf16[2,3072,192]{1,2,0:T(8,128)(2,1)}, u32[]{:S(2)}) copy-start(bf16[2,3072,192]{1,2,0:T(8,128)(2,1)} %param.11) | copy-start | bytes 7077892
  66.9 93.0 %all-to-all-start = ((bf16[8,640,768]{2,1,0:T(8,128)(2,1)}), bf16[8,640,768]{2,1,0:T(8,128)(2,1)}, u32[]{:S(2)}, u32[]{:S(2)}) async-start(bf16[8,640,768]{2,1,0:T(8,128)(2,1)} %broadcast_select_fusion), calls=%async_computation | async-start | bytes 15728640 | tf_op jit(solution)/shard_map/all_to_all | solution.py:55
  72.2 207.1 %all-gather.11.cloned.1.call-start = ((), (), s32[]{:S(2)}) async-start(), calls=%async_computation.4 | async-start | bytes 5898240 | tf_op jit(solution)/shard_map/all_gather | solution.py:52
  310.0 5.1 %copy-start.5 = (s32[4096,1]{0,1:T(1,128)S(1)}, s32[4096,1]{0,1:T(1,128)}, u32[]{:S(2)}) copy-start(s32[4096,1]{0,1:T(1,128)} %copy-done.4) | copy-start | bytes 49156
  310.0 92.7 %all-to-all-start.1 = ((bf16[8,640,768]{2,1,0:T(8,128)(2,1)}), bf16[8,640,768]{2,1,0:T(8,128)(2,1)}, u32[]{:S(2)}, u32[]{:S(2)}) async-start(bf16[8,640,768]{2,1,0:T(8,128)(2,1)} %bitcast.49), calls=%async_computation.1 | async-start | bytes 15728640 | tf_op jit(solution)/shard_map/all_to_all | solution.py:57
  402.7 23.3 %copy-start.6 = (pred[4096]{0:T(1024)(128)(4,1)S(1)}, pred[4096]{0:T(1024)(128)(4,1)}, u32[]{:S(2)}) copy-start(pred[4096]{0:T(1024)(128)(4,1)} %get-tuple-element.5) | copy-start | bytes 12292
  402.7 23.3 %copy-start.7 = (f32[4096,1]{0,1:T(1,128)S(1)}, f32[4096,1]{0,1:T(1,128)}, u32[]{:S(2)}) copy-start(f32[4096,1]{0,1:T(1,128)} %param.8) | copy-start | bytes 49156
  426.1 9.5 %copy-start.1 = (bf16[2,192,3072]{2,1,0:T(8,128)(2,1)S(1)}, bf16[2,192,3072]{2,1,0:T(8,128)(2,1)}, u32[]{:S(2)}) copy-start(bf16[2,192,3072]{2,1,0:T(8,128)(2,1)} %param.9) | copy-start | bytes 7077892
Sparse Core Ops, SparseCore 0:
  9.5 91.5 all-gather.6
  102.7 87.5 all-gather.8
  191.8 87.5 all-gather.10

commit v2 on v1

v2 whole, which is shorter than its diff:
```python
import functools

import jax
import jax.numpy as jnp
from jax import lax
from jax.experimental import pallas as pl
from jax.experimental.pallas import tpu as pltpu
from jax.sharding import PartitionSpec as P

MESH = pl.DeviceIdType.MESH
CHUNKS = 6
NZ = 4
PEERS = 8
LIGHT_AHEAD = 3
HEAVY_AHEAD = 2
VMEM_BYTES = 67_000_000


def capacity_rows(tok_rows, top_k, n_exp):
    return max(8, ((5 * top_k * tok_rows) // (4 * n_exp) + 7) // 8 * 8)


def moe_kernel(x_hbm, idx_ref, gate_ref, wg_hbm, wu_hbm, wd_hbm, out_hbm,
               wg_buf, wu_buf, wd_buf, wd_full, recv, sendb, back, acc, dest, dest_col, gate_col,
               w_recv, w_right, w_left, tok_recv, tok_send, ret_recv, ret_send, x_sem, go_sem, ready_sem):
    n_blk, blk = idx_ref.shape
    n_src, cap, d_model = recv.shape
    n_chunk, _, f_chunk = wg_buf.shape
    shard = d_model // NZ

    x = lax.axis_index("rep")
    z = lax.axis_index("data")
    p = lax.axis_index("expert")
    y, c = p // 2, p % 2
    me = 4 * y + 2 * c + x
    is_a = c == 0
    inner = jnp.logical_and(z > 0, z < NZ - 1)
    outer = jnp.logical_or(z == 0, z == NZ - 1)
    a_inner = jnp.logical_and(is_a, inner)

    def plane_id(dx, dy, cc):
        return (x + dx) % 2, (y + dy) % 2, cc

    def plane_dev(px, py, pc):
        return {"rep": px, "expert": 2 * py + pc}

    def plane_num(px, py, pc):
        return 4 * py + 2 * pc + px

    def w_view(j, s, m):
        if m == 0:
            return wg_buf.at[j, pl.ds(s * shard, shard), :]
        if m == 1:
            return wu_buf.at[j, pl.ds(s * shard, shard), :]
        return wd_buf.at[j, s]

    def w_local(j, m):
        if m == 2:
            src = wd_hbm.at[j]
        else:
            src = (wg_hbm, wu_hbm)[m].at[x, :, pl.ds(pl.multiple_of(j * f_chunk, f_chunk), f_chunk)]
        return pltpu.make_async_copy(src, w_view(j, z, m), w_recv.at[j, z, m])

    def w_send(j, s, m, right):
        view = w_view(j, s, m)
        return pltpu.make_async_remote_copy(
            src_ref=view, dst_ref=view,
            send_sem=(w_right if right else w_left).at[j, s, m], recv_sem=w_recv.at[j, s, m],
            device_id={"data": z + 1 if right else z - 1}, device_id_type=MESH)

    def own_start(j, right):
        for m in range(3):
            w_send(j, z, m, right).start()

    def own_light(j):
        @pl.when(z == 1)
        def _():
            own_start(j, True)

        @pl.when(z == 2)
        def _():
            own_start(j, False)

    def own_heavy(j):
        @pl.when(z == 1)
        def _():
            own_start(j, False)

        @pl.when(z == 2)
        def _():
            own_start(j, True)

    def own_outer():
        @pl.loop(0, n_chunk)
        def _(j):
            @pl.when(z == 0)
            def _():
                own_start(j, True)

            @pl.when(z == NZ - 1)
            def _():
                own_start(j, False)

    def event(j):
        @pl.when(jnp.logical_and(inner, j + LIGHT_AHEAD < n_chunk))
        def _():
            own_light(j + LIGHT_AHEAD)

        @pl.when(jnp.logical_and(inner, j + HEAVY_AHEAD < n_chunk))
        def _():
            own_heavy(j + HEAVY_AHEAD)

        for d in range(1, NZ):
            @pl.when(z - d >= 0)
            def _():
                for m in range(3):
                    w_send(j, z - d, m, True).wait_recv()

                    @pl.when(z < NZ - 1)
                    def _():
                        w_send(j, z - d, m, True).start()

            @pl.when(z + d < NZ)
            def _():
                for m in range(3):
                    w_send(j, z + d, m, False).wait_recv()

                    @pl.when(z > 0)
                    def _():
                        w_send(j, z + d, m, False).start()

    def wait_right(j):
        @pl.when(z < NZ - 1)
        def _():
            for d in range(NZ):
                @pl.when(z - d >= 0)
                def _():
                    for m in range(3):
                        w_send(j, z - d, m, True).wait_send()

    def wait_left(j):
        @pl.when(z > 0)
        def _():
            for d in range(NZ):
                @pl.when(z + d < NZ)
                def _():
                    for m in range(3):
                        w_send(j, z + d, m, False).wait_send()

    def go(right):
        @pl.loop(0, n_chunk - 1)
        def _(j):
            (wait_right if right else wait_left)(j)

        pl.semaphore_signal(go_sem.at[0 if right else 1], inc=1, device_id={"expert": p + 1}, device_id_type=MESH)

    def x_load(b, dst):
        return pltpu.make_async_copy(x_hbm.at[pl.ds(pl.multiple_of(b * blk, blk), blk), :], dst.at[b, pl.ds(0, blk), :], x_sem.at[b])

    @pl.loop(0, n_blk)
    def _(b):
        x_load(b, back).start()

    @pl.loop(0, n_chunk)
    def _(j):
        for m in range(3):
            w_local(j, m).start()

    barrier = pltpu.get_barrier_semaphore()
    for k in range(1, PEERS):
        dev = plane_dev(*plane_id(k % 2, (k // 2) % 2, (c + k // 4) % 2))
        pl.semaphore_signal(barrier, inc=1, device_id=dev, device_id_type=MESH)

    @pl.when(z > 0)
    def _():
        pl.semaphore_signal(barrier, inc=1, device_id={"data": z - 1}, device_id_type=MESH)

    @pl.when(z < NZ - 1)
    def _():
        pl.semaphore_signal(barrier, inc=1, device_id={"data": z + 1}, device_id_type=MESH)

    @pl.when(outer)
    def _():
        pl.semaphore_wait(barrier, PEERS)

    @pl.when(inner)
    def _():
        pl.semaphore_wait(barrier, PEERS + 1)

    @pl.loop(0, n_chunk)
    def _(j):
        for m in range(3):
            w_local(j, m).wait()

    @pl.when(is_a)
    def _():
        @pl.when(outer)
        def _():
            own_outer()

        @pl.when(inner)
        def _():
            for j in range(LIGHT_AHEAD):
                own_light(j)
            for j in range(HEAVY_AHEAD):
                own_heavy(j)

    tri = (lax.broadcasted_iota(jnp.int32, (blk, blk), 0) < lax.broadcasted_iota(jnp.int32, (blk, blk), 1)).astype(jnp.float32).astype(jnp.bfloat16)
    eye = lax.broadcasted_iota(jnp.int32, (blk, blk), 0) == lax.broadcasted_iota(jnp.int32, (blk, blk), 1)
    running = jnp.zeros((16, 1), jnp.float32)
    for b in range(n_blk):
        ids = idx_ref[b:b + 1, :]
        one_hot = (lax.broadcasted_iota(jnp.int32, (16, blk), 0) == ids).astype(jnp.float32)
        before = jnp.dot(one_hot.astype(jnp.bfloat16), tri, preferred_element_type=jnp.float32) + running
        slot = jnp.sum(one_hot * before, axis=0, keepdims=True)
        running = running + jnp.sum(one_hot, axis=1, keepdims=True)
        row = jnp.where(slot < cap, ids.astype(jnp.float32) * cap + slot, -1.0)
        dest[b:b + 1, :] = row.astype(jnp.int32)
        dest_col[b] = jnp.sum(jnp.where(eye, row, 0.0), axis=1, keepdims=True).astype(jnp.int32)
        gate_col[b] = jnp.sum(jnp.where(eye, gate_ref[b:b + 1, :], 0.0), axis=1, keepdims=True)

    @pl.loop(0, n_blk)
    def _(b):
        x_load(b, back).wait()

    def tok_copy(e, dev):
        return pltpu.make_async_remote_copy(
            src_ref=sendb.at[e], dst_ref=recv.at[me], send_sem=tok_send.at[e], recv_sem=tok_recv.at[me],
            device_id=dev, device_id_type=MESH)

    @pl.loop(0, PEERS)
    def _(k):
        kk = k % 4
        peer = plane_id((kk + 1) % 2, ((kk + 1) // 2) % 2, k // 4)
        e = plane_num(*peer)
        slots = lax.broadcasted_iota(jnp.int32, (cap, blk), 0) + e * cap

        def pick(b):
            hot = (slots == dest[pl.ds(b, 1), :]).astype(jnp.float32).astype(jnp.bfloat16)
            return jnp.dot(hot, back[b, 0:blk, :], preferred_element_type=jnp.float32)

        acc[0] = pick(0)

        @pl.loop(1, n_blk - 1)
        def _(b):
            acc[0] += pick(b)

        rows = (acc[0] + pick(n_blk - 1)).astype(jnp.bfloat16)

        @pl.when(e == me)
        def _():
            recv[me] = rows

        @pl.when(e != me)
        def _():
            sendb[e] = rows
            tok_copy(e, plane_dev(*peer)).start()

        for kq, ev in ((2, 0), (5, 1), (7, 2)):
            @pl.when(jnp.logical_and(a_inner, k == kq))
            def _():
                event(ev)

    for k in range(1, PEERS):
        dev = plane_dev(*plane_id(k % 2, (k // 2) % 2, (c + k // 4) % 2))
        pl.semaphore_signal(ready_sem, inc=1, device_id=dev, device_id_type=MESH)

    @pl.loop(0, n_src)
    def _(s):
        acc[s] = jnp.zeros((cap, d_model), jnp.float32)

    @pl.when(is_a)
    def _():
        @pl.when(inner)
        def _():
            @pl.loop(3, n_chunk)
            def _(j):
                event(j)

        @pl.when(z == 0)
        def _():
            go(True)

        @pl.when(z == NZ - 1)
        def _():
            go(False)

    @pl.when(c == 1)
    def _():
        @pl.when(z < 2)
        def _():
            pl.semaphore_wait(go_sem.at[0], 1)

        @pl.when(z >= 2)
        def _():
            pl.semaphore_wait(go_sem.at[1], 1)

        @pl.when(outer)
        def _():
            own_outer()

        @pl.when(inner)
        def _():
            for j in range(LIGHT_AHEAD):
                own_light(j)

            @pl.when(z == 1)
            def _():
                pl.semaphore_wait(go_sem.at[1], 1)

            @pl.when(z == 2)
            def _():
                pl.semaphore_wait(go_sem.at[0], 1)

            for j in range(HEAVY_AHEAD):
                own_heavy(j)
            event(0)
            event(1)

    for k in range(1, PEERS):
        peer = plane_id(k % 2, (k // 2) % 2, (c + k // 4) % 2)
        s = plane_num(*peer)
        pltpu.make_async_remote_copy(
            src_ref=sendb.at[s], dst_ref=recv.at[s], send_sem=tok_send.at[s], recv_sem=tok_recv.at[s],
            device_id=plane_dev(*peer), device_id_type=MESH).wait_recv()

    def load_down(j):
        for s in range(NZ):
            piece = wd_buf[j, s]
            wd_full[0:f_chunk // 2, s * shard:(s + 1) * shard] = piece[:, :shard]
            wd_full[f_chunk // 2:f_chunk, s * shard:(s + 1) * shard] = piece[:, shard:]

    def ffn(j, s):
        rows = recv[s]
        g = jnp.dot(rows, wg_buf[j], preferred_element_type=jnp.float32)
        u = jnp.dot(rows, wu_buf[j], preferred_element_type=jnp.float32)
        h = (g * jax.nn.sigmoid(g) * u).astype(jnp.bfloat16)
        return jnp.dot(h, wd_full[...], preferred_element_type=jnp.float32)

    def before_chunk(j):
        @pl.when(outer)
        def _():
            event(j)

        @pl.when(jnp.logical_and(jnp.logical_and(c == 1, inner), j + 2 < n_chunk))
        def _():
            event(j + 2)

        load_down(j)

    @pl.loop(0, n_chunk - 1)
    def _(j):
        before_chunk(j)

        @pl.loop(0, n_src)
        def _(s):
            acc[s] += ffn(j, s)

        @pl.when(jnp.logical_and(a_inner, j == 0))
        def _():
            @pl.when(z == 1)
            def _():
                go(True)

            @pl.when(z == 2)
            def _():
                go(False)

        @pl.when(jnp.logical_and(a_inner, j == 1))
        def _():
            @pl.when(z == 1)
            def _():
                go(False)

            @pl.when(z == 2)
            def _():
                go(True)

    before_chunk(n_chunk - 1)
    for k in range(1, PEERS):
        peer = plane_id(k % 2, (k // 2) % 2, (c + k // 4) % 2)
        tok_copy(plane_num(*peer), plane_dev(*peer)).wait_send()
    pl.semaphore_wait(ready_sem, PEERS - 1)

    def ret_copy(s, dev):
        return pltpu.make_async_remote_copy(
            src_ref=sendb.at[s], dst_ref=back.at[me], send_sem=ret_send.at[s], recv_sem=ret_recv.at[me],
            device_id=dev, device_id_type=MESH)

    @pl.loop(0, PEERS)
    def _(r):
        q, rr = r // 4, r % 4
        peer = plane_id((1 - q) * ((rr + 1) % 2) + q * (1 - rr // 2), (1 - q) * (rr % 2) + q * (1 - rr // 2), (c + rr // 2 + q * rr) % 2)
        s = plane_num(*peer)
        rows = (acc[s] + ffn(n_chunk - 1, s)).astype(jnp.bfloat16)

        @pl.when(s == me)
        def _():
            back[me] = rows

        @pl.when(s != me)
        def _():
            sendb[s] = rows
            ret_copy(s, plane_dev(*peer)).start()

    @pl.loop(0, n_blk)
    def _(b):
        x_load(b, recv).start()

    @pl.loop(0, n_blk)
    def _(b):
        acc[b, 0:blk, :] = jnp.zeros((blk, d_model), jnp.float32)

    def arrived(k):
        kk = k % 4
        peer = plane_id((kk // 2 + kk + 1) % 2, kk % 2, k // 4)
        e = plane_num(*peer)

        @pl.when(e != me)
        def _():
            pltpu.make_async_remote_copy(
                src_ref=sendb.at[e], dst_ref=back.at[e], send_sem=ret_send.at[e], recv_sem=ret_recv.at[e],
                device_id=plane_dev(*peer), device_id_type=MESH).wait_recv()

        return e

    def put_back(e, b):
        hot = (lax.broadcasted_iota(jnp.int32, (blk, cap), 1) + e * cap == dest_col[b]).astype(jnp.float32).astype(jnp.bfloat16)
        return jnp.dot(hot, back[e], preferred_element_type=jnp.float32)

    @pl.loop(0, PEERS - 1)
    def _(k):
        e = arrived(k)

        @pl.loop(0, n_blk)
        def _(b):
            acc[b, 0:blk, :] += put_back(e, b)

    @pl.loop(0, n_blk)
    def _(b):
        x_load(b, recv).wait()

    e_last = arrived(PEERS - 1)

    def out_copy(b):
        return pltpu.make_async_copy(recv.at[b, pl.ds(0, blk), :], out_hbm.at[pl.ds(pl.multiple_of(b * blk, blk), blk), :], x_sem.at[b])

    @pl.loop(0, n_blk)
    def _(b):
        mixed = (acc[b, 0:blk, :] + put_back(e_last, b)) * gate_col[b]
        recv[b, 0:blk, :] = (recv[b, 0:blk, :].astype(jnp.float32) + mixed).astype(jnp.bfloat16)
        out_copy(b).start()

    @pl.when(is_a)
    def _():
        wait_right(n_chunk - 1)
        wait_left(n_chunk - 1)

    @pl.when(c == 1)
    def _():
        @pl.loop(0, n_chunk)
        def _(j):
            wait_right(j)
            wait_left(j)

    for k in range(1, PEERS):
        peer = plane_id(k % 2, (k // 2) % 2, (c + k // 4) % 2)
        ret_copy(plane_num(*peer), plane_dev(*peer)).wait_send()

    @pl.loop(0, n_blk)
    def _(b):
        out_copy(b).wait()


def solution(mesh):
    n_group = mesh.shape["expert"]
    tok_spec = P(("rep", "expert", "data"), None)
    wide_spec = P("expert", "data", None)
    down_spec = P("expert", None, "data")

    def device_step(x_loc, idx_loc, gate_loc, wg_loc, wu_loc, wd_loc):
        tok_rows, d_model = x_loc.shape
        top_k = idx_loc.shape[1]
        n_exp = wg_loc.shape[0] * n_group
        ffn = wg_loc.shape[2]
        cap = capacity_rows(tok_rows, top_k, n_exp)
        blk = tok_rows // PEERS
        f_chunk = ffn // CHUNKS
        shard = d_model // NZ
        wd_own = lax.dynamic_index_in_dim(wd_loc, lax.axis_index("rep"), 0, False)
        wd_own = wd_own.reshape(CHUNKS, 2, f_chunk // 2, shard).transpose(0, 2, 1, 3).reshape(CHUNKS, f_chunk // 2, 2 * shard)
        any_spec = pl.BlockSpec(memory_space=pl.ANY)
        vmem_spec = pl.BlockSpec(memory_space=pltpu.VMEM)
        dma = pltpu.SemaphoreType.DMA
        return pl.pallas_call(
            moe_kernel,
            out_shape=jax.ShapeDtypeStruct((tok_rows, d_model), jnp.bfloat16),
            in_specs=[any_spec, vmem_spec, vmem_spec, any_spec, any_spec, any_spec],
            out_specs=any_spec,
            scratch_shapes=[
                pltpu.VMEM((CHUNKS, d_model, f_chunk), jnp.bfloat16),
                pltpu.VMEM((CHUNKS, d_model, f_chunk), jnp.bfloat16),
                pltpu.VMEM((CHUNKS, NZ, f_chunk // 2, 2 * shard), jnp.bfloat16),
                pltpu.VMEM((f_chunk, d_model), jnp.bfloat16),
                pltpu.VMEM((PEERS, cap, d_model), jnp.bfloat16),
                pltpu.VMEM((PEERS, cap, d_model), jnp.bfloat16),
                pltpu.VMEM((PEERS, cap, d_model), jnp.bfloat16),
                pltpu.VMEM((PEERS, cap, d_model), jnp.float32),
                pltpu.VMEM((PEERS, blk), jnp.int32),
                pltpu.VMEM((PEERS, blk, 1), jnp.int32),
                pltpu.VMEM((PEERS, blk, 1), jnp.float32),
                dma((CHUNKS, NZ, 3)), dma((CHUNKS, NZ, 3)), dma((CHUNKS, NZ, 3)),
                dma((PEERS,)), dma((PEERS,)), dma((PEERS,)), dma((PEERS,)), dma((PEERS,)),
                pltpu.SemaphoreType.REGULAR((2,)), pltpu.SemaphoreType.REGULAR,
            ],
            compiler_params=pltpu.CompilerParams(collective_id=0, has_side_effects=True, vmem_limit_bytes=VMEM_BYTES),
        )(x_loc, idx_loc.reshape(PEERS, blk), gate_loc.reshape(PEERS, blk), wg_loc, wu_loc, wd_own)

    return jax.shard_map(device_step, mesh=mesh, in_specs=(tok_spec, tok_spec, tok_spec, wide_spec, wide_spec, down_spec), out_specs=tok_spec, check_vma=False)
```

time: 443 us -> 390 us (0.88)
  the two profiles are of different devices: /device:TPU:0 before, /device:TPU:15 now
where the time goes in v2:
time: 390 us; the launch traced here: 389 us
  Pallas kernels  375 us (96%)
  local copies, waits for them, and re-layouts  11.9 us (3%)
    pallas_call x1, Pallas kernels, device_step(): pl.pallas_call(moe_kernel, out_shape=jax.ShapeDtypeStruct((tok_rows, d_mo...  375 us

profile of v2, /device:TPU:15, one launch (start us, length us, event | category | flops | bytes accessed | tf_op | source)
XLA Modules:
  0.0 389.5 jit_solution(12967893448685612414)
XLA Ops:
  0.0 0.5 broadcast.6
  0.5 1.4 reduce.6
  1.9 0.6 reshape.13.idx_ref
  2.5 0.5 broadcast.7
  3.0 1.4 reduce.7
  4.4 0.6 reshape.14.gate_ref
  5.0 1.3 constant_dynamic-slice_fusion
  6.4 0.9 reshape.15
  7.3 0.2 copy.7
  7.5 1.4 copy.8.wd_hbm
  8.9 374.7 %shard_map.64 = bf16[4096,768]{1,0:T(8,128)(2,1)} custom-call(bf16[4096,768]{1,0:T(8,128)(2,1)} %x_hbm.1, s32[8,512]{1,0:T(8,128)} %reshape.13.idx_ref, f32[8,512]{1,0:T(8,128)} %reshape.14.gate_ref, bf16[2,192,3072]{2,1,0:T(8,128)(2,1)} %wg_hbm.1, bf16[2,192,3072]{2,1,0:T(8,128)(2,1)} %wu_hbm.1, bf16[6,256,384]{2,1,0:T(8,128)(2,1)} %copy.8.wd_hbm), custom_call_target="tpu_custom_call" | custom-call | tf_op jit(solution)/shard_map/pallas_call | solution.py:495
  383.6 5.9 %copy.10 = bf16[4096,768]{1,0:T(8,128)(2,1)} copy(bf16[4096,768]{1,0:T(8,128)(2,1)} %shard_map.64) | data formatting | bytes 12582912

commit v3 on v2

v3 whole, which is shorter than its diff:
```python
import functools

import jax
import jax.numpy as jnp
from jax import lax
from jax.experimental import pallas as pl
from jax.experimental.pallas import tpu as pltpu
from jax.sharding import PartitionSpec as P

MESH = pl.DeviceIdType.MESH
CHUNKS = 6
NZ = 4
PEERS = 8
AHEAD = 3
VMEM_BYTES = 67_000_000


def capacity_rows(tok_rows, top_k, n_exp):
    return max(8, ((5 * top_k * tok_rows) // (4 * n_exp) + 7) // 8 * 8)


def moe_kernel(x_hbm, idx_ref, gate_ref, wg_hbm, wu_hbm, wd_hbm, out_hbm,
               wg_buf, wu_buf, wd_buf, recv, sendb, back, acc, dest, dest_col, gate_col,
               w_recv, w_light, w_heavy, tok_recv, tok_send, ret_recv, ret_send, x_sem, go_sem, ready_sem):
    n_src, cap, d_model = recv.shape
    n_blk, _, _ = dest_col.shape
    blk = dest_col.shape[1]
    n_chunk, _, f_chunk = wg_buf.shape
    shard = d_model // NZ

    x = lax.axis_index("rep")
    z = lax.axis_index("data")
    p = lax.axis_index("expert")
    y, c = p // 2, p % 2
    me = 4 * c + 2 * y + x
    is_a = c == 0
    inner = jnp.logical_and(z > 0, z < NZ - 1)
    outer = jnp.logical_or(z == 0, z == NZ - 1)
    a_inner = jnp.logical_and(is_a, inner)

    def plane_id(dx, dy, cc):
        return (x + dx) % 2, (y + dy) % 2, cc

    def plane_dev(px, py, pc):
        return {"rep": px, "expert": 2 * py + pc}

    def plane_num(px, py, pc):
        return 4 * pc + 2 * py + px

    def w_view(j, s, m):
        return (wg_buf, wu_buf, wd_buf)[m].at[j, pl.ds(s * shard, shard), :]

    def w_local(j, m):
        src = (wg_hbm, wu_hbm, wd_hbm)[m].at[x, :, pl.ds(pl.multiple_of(j * f_chunk, f_chunk), f_chunk)]
        return pltpu.make_async_copy(src, w_view(j, z, m), w_recv.at[j, z, m])

    def w_copy(j, s, m, heavy, dev):
        view = w_view(j, s, m)
        return pltpu.make_async_remote_copy(
            src_ref=view, dst_ref=view, send_sem=(w_heavy if heavy else w_light).at[j, s, m], recv_sem=w_recv.at[j, s, m],
            device_id={"data": dev}, device_id_type=MESH)

    end, far, mate = 3 * (z - 1), 3 * (2 - z), 3 - z

    def pass_on(j, s, heavy, arrives=True):
        for m in range(3):
            cp = w_copy(j, s, m, heavy, end if heavy else mate)
            if arrives:
                cp.wait_recv()
            cp.start()

    def light_own(j):
        pass_on(j, z, False, False)

    def light_end(j):
        pass_on(j, end, False)

    def heavy_own(j):
        pass_on(j, z, True, False)

    def heavy_mate(j):
        pass_on(j, mate, True)

    def heavy_far(j):
        pass_on(j, far, True)

    def heavy_all(j):
        heavy_own(j)
        heavy_mate(j)
        heavy_far(j)

    def own_outer():
        @pl.loop(0, n_chunk)
        def _(j):
            for m in range(3):
                w_copy(j, z, m, False, (z + 3) // 3).start()

    def end_wait(j):
        for d in range(1, NZ):
            for m in range(3):
                w_copy(j, (z + d) % NZ, m, False, (z + 3) // 3).wait_recv()

    def sent(j, shards, heavy):
        for s in shards:
            for m in range(3):
                w_copy(j, s, m, heavy, (z + 1) % NZ).wait_send()

    def sent_outer(j):
        sent(j, (z,), False)

    def sent_light(j):
        sent(j, (z, end), False)

    def sent_heavy(j):
        sent(j, (z, mate, far), True)

    def go(done, heavy):
        @pl.loop(0, n_chunk - 1)
        def _(j):
            done(j)

        pl.semaphore_signal(go_sem.at[heavy], inc=1, device_id={"expert": p + 1}, device_id_type=MESH)

    def x_load(b, dst):
        return pltpu.make_async_copy(x_hbm.at[pl.ds(pl.multiple_of(b * blk, blk), blk), :], dst.at[b, pl.ds(0, blk), :], x_sem.at[b])

    @pl.loop(0, n_blk)
    def _(b):
        x_load(b, back).start()

    @pl.loop(0, n_chunk)
    def _(j):
        for m in range(3):
            w_local(j, m).start()

    barrier = pltpu.get_barrier_semaphore()
    for k in range(1, PEERS):
        dev = plane_dev(*plane_id(k % 2, (k // 2) % 2, (c + k // 4) % 2))
        pl.semaphore_signal(barrier, inc=1, device_id=dev, device_id_type=MESH)

    @pl.when(z > 0)
    def _():
        pl.semaphore_signal(barrier, inc=1, device_id={"data": z - 1}, device_id_type=MESH)

    @pl.when(z < NZ - 1)
    def _():
        pl.semaphore_signal(barrier, inc=1, device_id={"data": z + 1}, device_id_type=MESH)

    @pl.when(outer)
    def _():
        pl.semaphore_wait(barrier, PEERS)

    @pl.when(inner)
    def _():
        pl.semaphore_wait(barrier, PEERS + 1)

    @pl.loop(0, n_chunk)
    def _(j):
        for m in range(3):
            w_local(j, m).wait()

    @pl.when(is_a)
    def _():
        @pl.when(outer)
        def _():
            own_outer()

        @pl.when(inner)
        def _():
            for j in range(AHEAD):
                light_own(j)
                heavy_own(j)

    tri = (lax.broadcasted_iota(jnp.int32, (blk, blk), 0) < lax.broadcasted_iota(jnp.int32, (blk, blk), 1)).astype(jnp.float32).astype(jnp.bfloat16)
    eye = lax.broadcasted_iota(jnp.int32, (blk, blk), 0) == lax.broadcasted_iota(jnp.int32, (blk, blk), 1)
    running = jnp.zeros((16, 1), jnp.float32)
    for b in range(n_blk):
        ids = idx_ref[:, b * blk:(b + 1) * blk]
        ids = (ids // 2 % 2) * 4 + (ids // 4) * 2 + ids % 2
        one_hot = (lax.broadcasted_iota(jnp.int32, (16, blk), 0) == ids).astype(jnp.float32)
        before = jnp.dot(one_hot.astype(jnp.bfloat16), tri, preferred_element_type=jnp.float32) + running
        slot = jnp.sum(one_hot * before, axis=0, keepdims=True)
        running = running + jnp.sum(one_hot, axis=1, keepdims=True)
        row = jnp.where(slot < cap, ids.astype(jnp.float32) * cap + slot, -1.0)
        dest[b:b + 1, :] = row.astype(jnp.int32)
        dest_col[b] = jnp.sum(jnp.where(eye, row, 0.0), axis=1, keepdims=True).astype(jnp.int32)
        gate_col[b] = jnp.sum(jnp.where(eye, gate_ref[:, b * blk:(b + 1) * blk], 0.0), axis=1, keepdims=True)

    @pl.loop(0, n_blk)
    def _(b):
        x_load(b, back).wait()

    def tok_copy(e, dev):
        return pltpu.make_async_remote_copy(
            src_ref=sendb.at[e], dst_ref=recv.at[me], send_sem=tok_send.at[e], recv_sem=tok_recv.at[me],
            device_id=dev, device_id_type=MESH)

    @pl.loop(0, PEERS)
    def _(k):
        kk = k % 4
        peer = plane_id((kk + 1) % 2, ((kk + 1) // 2) % 2, k // 4)
        e = plane_num(*peer)
        slots = lax.broadcasted_iota(jnp.int32, (cap, blk), 0) + e * cap

        def pick(b):
            hot = (slots == dest[pl.ds(b, 1), :]).astype(jnp.float32).astype(jnp.bfloat16)
            return jnp.dot(hot, back[b, 0:blk, :], preferred_element_type=jnp.float32)

        acc[0] = pick(0)

        @pl.loop(1, n_blk - 1)
        def _(b):
            acc[0] += pick(b)

        rows = (acc[0] + pick(n_blk - 1)).astype(jnp.bfloat16)

        @pl.when(e == me)
        def _():
            recv[me] = rows

        @pl.when(e != me)
        def _():
            sendb[e] = rows
            tok_copy(e, plane_dev(*peer)).start()

        def at(step):
            return pl.when(jnp.logical_and(a_inner, k == step))

        @at(1)
        def _():
            light_end(0)
            light_own(3)

        @at(2)
        def _():
            light_end(1)
            light_own(4)
            heavy_mate(0)
            heavy_mate(1)
            heavy_own(3)

        @at(3)
        def _():
            light_end(2)
            light_own(5)

        @at(4)
        def _():
            light_end(3)
            heavy_mate(2)
            heavy_far(0)
            heavy_own(4)

        @at(5)
        def _():
            light_end(4)

        @at(6)
        def _():
            light_end(5)
            heavy_mate(3)
            heavy_far(1)
            heavy_own(5)

        @pl.when(jnp.logical_and(jnp.logical_and(is_a, outer), k == 6))
        def _():
            go(sent_outer, 0)

    for k in range(1, PEERS):
        dev = plane_dev(*plane_id(k % 2, (k // 2) % 2, (c + k // 4) % 2))
        pl.semaphore_signal(ready_sem, inc=1, device_id=dev, device_id_type=MESH)

    @pl.loop(0, n_src)
    def _(s):
        acc[s] = jnp.zeros((cap, d_model), jnp.float32)

    @pl.when(a_inner)
    def _():
        heavy_mate(4)
        heavy_far(2)

    @pl.when(c == 1)
    def _():
        pl.semaphore_wait(go_sem.at[0], 1)

        @pl.when(outer)
        def _():
            own_outer()

        @pl.when(inner)
        def _():
            @pl.loop(0, n_chunk)
            def _(j):
                light_own(j)
                light_end(j)

            pl.semaphore_wait(go_sem.at[1], 1)

            @pl.loop(0, 3)
            def _(j):
                heavy_all(j)

    for k in range(1, PEERS):
        peer = plane_id(k % 2, (k // 2) % 2, (c + k // 4) % 2)
        s = plane_num(*peer)
        pltpu.make_async_remote_copy(
            src_ref=sendb.at[s], dst_ref=recv.at[s], send_sem=tok_send.at[s], recv_sem=tok_recv.at[s],
            device_id=plane_dev(*peer), device_id_type=MESH).wait_recv()

    @pl.when(a_inner)
    def _():
        heavy_mate(5)

    def ffn(j, s):
        rows = recv[s]
        g = jnp.dot(rows, wg_buf[j], preferred_element_type=jnp.float32)
        u = jnp.dot(rows, wu_buf[j], preferred_element_type=jnp.float32)
        h = (g * jax.nn.sigmoid(g) * u).astype(jnp.bfloat16)
        return lax.dot_general(h, wd_buf[j], (((1,), (1,)), ((), ())), preferred_element_type=jnp.float32)

    def before_chunk(j):
        @pl.when(outer)
        def _():
            end_wait(j)

    @pl.loop(0, n_chunk - 1)
    def _(j):
        before_chunk(j)

        @pl.loop(0, n_src)
        def _(s):
            acc[s] += ffn(j, s)

        @pl.when(jnp.logical_and(a_inner, j == 0))
        def _():
            heavy_far(3)
            heavy_far(4)
            go(sent_light, 0)

        @pl.when(jnp.logical_and(a_inner, j == 1))
        def _():
            heavy_far(5)

        @pl.when(jnp.logical_and(a_inner, j == 2))
        def _():
            go(sent_heavy, 1)

        @pl.when(jnp.logical_and(jnp.logical_and(c == 1, inner), j < 3))
        def _():
            heavy_all(j + 3)

    before_chunk(n_chunk - 1)
    for k in range(1, PEERS):
        peer = plane_id(k % 2, (k // 2) % 2, (c + k // 4) % 2)
        tok_copy(plane_num(*peer), plane_dev(*peer)).wait_send()
    pl.semaphore_wait(ready_sem, PEERS - 1)

    def ret_copy(s, dev):
        return pltpu.make_async_remote_copy(
            src_ref=sendb.at[s], dst_ref=back.at[me], send_sem=ret_send.at[s], recv_sem=ret_recv.at[me],
            device_id=dev, device_id_type=MESH)

    @pl.loop(0, PEERS)
    def _(r):
        q, rr = r // 4, r % 4
        peer = plane_id((1 - q) * ((rr + 1) % 2) + q * (1 - rr // 2), (1 - q) * (rr % 2) + q * (1 - rr // 2), (c + rr // 2 + q * rr) % 2)
        s = plane_num(*peer)
        rows = (acc[s] + ffn(n_chunk - 1, s)).astype(jnp.bfloat16)

        @pl.when(s == me)
        def _():
            back[me] = rows

        @pl.when(s != me)
        def _():
            sendb[s] = rows
            ret_copy(s, plane_dev(*peer)).start()

    @pl.loop(0, n_blk)
    def _(b):
        x_load(b, recv).start()

    @pl.loop(0, n_blk)
    def _(b):
        acc[b, 0:blk, :] = jnp.zeros((blk, d_model), jnp.float32)

    def arrived(k):
        py, pc = (y + k) % 2, k // 2
        for dx in range(2):
            peer = ((x + dx) % 2, py, pc)
            e = plane_num(*peer)

            @pl.when(e != me)
            def _():
                pltpu.make_async_remote_copy(
                    src_ref=sendb.at[e], dst_ref=back.at[e], send_sem=ret_send.at[e], recv_sem=ret_recv.at[e],
                    device_id=plane_dev(*peer), device_id_type=MESH).wait_recv()

        return 4 * pc + 2 * py

    def put_back(e, b):
        hot = (lax.broadcasted_iota(jnp.int32, (blk, 2 * cap), 1) + e * cap == dest_col[b]).astype(jnp.float32).astype(jnp.bfloat16)
        rows = back[pl.ds(e, 2)].reshape(2 * cap, d_model)
        return jnp.dot(hot, rows, preferred_element_type=jnp.float32)

    @pl.loop(0, PEERS // 2 - 1)
    def _(k):
        e = arrived(k)

        @pl.loop(0, n_blk)
        def _(b):
            acc[b, 0:blk, :] += put_back(e, b)

    @pl.loop(0, n_blk)
    def _(b):
        x_load(b, recv).wait()

    e_last = arrived(PEERS // 2 - 1)

    def out_copy(b):
        return pltpu.make_async_copy(recv.at[b, pl.ds(0, blk), :], out_hbm.at[pl.ds(pl.multiple_of(b * blk, blk), blk), :], x_sem.at[b])

    @pl.loop(0, n_blk)
    def _(b):
        mixed = (acc[b, 0:blk, :] + put_back(e_last, b)) * gate_col[b]
        recv[b, 0:blk, :] = (recv[b, 0:blk, :].astype(jnp.float32) + mixed).astype(jnp.bfloat16)
        out_copy(b).start()

    @pl.loop((n_chunk - 1) * (1 - c), n_chunk)
    def _(j):
        @pl.when(outer)
        def _():
            sent_outer(j)

        @pl.when(inner)
        def _():
            sent_light(j)
            sent_heavy(j)

    for k in range(1, PEERS):
        peer = plane_id(k % 2, (k // 2) % 2, (c + k // 4) % 2)
        ret_copy(plane_num(*peer), plane_dev(*peer)).wait_send()

    @pl.loop(0, n_blk)
    def _(b):
        out_copy(b).wait()


def solution(mesh):
    n_group = mesh.shape["expert"]
    tok_spec = P(("rep", "expert", "data"), None)
    wide_spec = P("expert", "data", None)
    down_spec = P("expert", None, "data")

    def device_step(x_loc, idx_loc, gate_loc, wg_loc, wu_loc, wd_loc):
        tok_rows, d_model = x_loc.shape
        top_k = idx_loc.shape[1]
        n_exp = wg_loc.shape[0] * n_group
        ffn = wg_loc.shape[2]
        cap = capacity_rows(tok_rows, top_k, n_exp)
        blk = tok_rows // PEERS
        f_chunk = ffn // CHUNKS
        any_spec = pl.BlockSpec(memory_space=pl.ANY)
        vmem_spec = pl.BlockSpec(memory_space=pltpu.VMEM)
        dma = pltpu.SemaphoreType.DMA
        return pl.pallas_call(
            moe_kernel,
            out_shape=jax.ShapeDtypeStruct((tok_rows, d_model), jnp.bfloat16),
            in_specs=[any_spec, vmem_spec, vmem_spec, any_spec, any_spec, any_spec],
            out_specs=any_spec,
            scratch_shapes=[
                pltpu.VMEM((CHUNKS, d_model, f_chunk), jnp.bfloat16),
                pltpu.VMEM((CHUNKS, d_model, f_chunk), jnp.bfloat16),
                pltpu.VMEM((CHUNKS, d_model, f_chunk), jnp.bfloat16),
                pltpu.VMEM((PEERS, cap, d_model), jnp.bfloat16),
                pltpu.VMEM((PEERS, cap, d_model), jnp.bfloat16),
                pltpu.VMEM((PEERS, cap, d_model), jnp.bfloat16),
                pltpu.VMEM((PEERS, cap, d_model), jnp.float32),
                pltpu.VMEM((PEERS, blk), jnp.int32),
                pltpu.VMEM((PEERS, blk, 1), jnp.int32),
                pltpu.VMEM((PEERS, blk, 1), jnp.float32),
                dma((CHUNKS, NZ, 3)), dma((CHUNKS, NZ, 3)), dma((CHUNKS, NZ, 3)),
                dma((PEERS,)), dma((PEERS,)), dma((PEERS,)), dma((PEERS,)), dma((PEERS,)),
                pltpu.SemaphoreType.REGULAR((2,)), pltpu.SemaphoreType.REGULAR,
            ],
            compiler_params=pltpu.CompilerParams(collective_id=0, has_side_effects=True, vmem_limit_bytes=VMEM_BYTES),
        )(x_loc, idx_loc.T, gate_loc.T, wg_loc, wu_loc, wd_loc.transpose(0, 2, 1))

    return jax.shard_map(device_step, mesh=mesh, in_specs=(tok_spec, tok_spec, tok_spec, wide_spec, wide_spec, down_spec), out_specs=tok_spec, check_vma=False)
```

time: 390 us -> 304 us (0.78)
  the two profiles are of different devices: /device:TPU:15 before, /device:TPU:0 now
where the time goes in v3:
time: 304 us
  Pallas kernels  298 us (98%)
  local copies, waits for them, and re-layouts  5.89 us (2%)
    pallas_call x1, Pallas kernels, device_step(): pl.pallas_call(moe_kernel, out_shape=jax.ShapeDtypeStruct((tok_rows, d_mo...  298 us

profile of v3, /device:TPU:0, one launch (start us, length us, event | category | flops | bytes accessed | tf_op | source)
XLA Modules:
  0.0 303.9 jit_solution(12455389741879271763)
XLA Ops:
  0.0 298.0 %shard_map.64 = bf16[4096,768]{1,0:T(8,128)(2,1)} custom-call(bf16[4096,768]{1,0:T(8,128)(2,1)} %x_hbm.1, s32[1,4096]{1,0:T(1,128)} %bitcast.4, f32[1,4096]{1,0:T(1,128)} %bitcast.5, bf16[2,192,3072]{2,1,0:T(8,128)(2,1)} %wg_hbm.1, bf16[2,192,3072]{2,1,0:T(8,128)(2,1)} %wu_hbm.1, bf16[2,192,3072]{2,1,0:T(8,128)(2,1)} %bitcast.3), custom_call_target="tpu_custom_call" | custom-call | tf_op jit(solution)/shard_map/pallas_call | solution.py:466
  298.0 5.9 %copy.8 = bf16[4096,768]{1,0:T(8,128)(2,1)} copy(bf16[4096,768]{1,0:T(8,128)(2,1)} %shard_map.64) | data formatting | bytes 12582912

commit v4 on v3

--- a/solution.py
+++ b/solution.py
@@ -19,12 +19,17 @@
     return max(8, ((5 * top_k * tok_rows) // (4 * n_exp) + 7) // 8 * 8)
 
 
-def moe_kernel(x_hbm, idx_ref, gate_ref, wg_hbm, wu_hbm, wd_hbm, out_hbm,
-               wg_buf, wu_buf, wd_buf, recv, sendb, back, acc, dest, dest_col, gate_col,
-               w_recv, w_light, w_heavy, tok_recv, tok_send, ret_recv, ret_send, x_sem, go_sem, ready_sem):
-    n_src, cap, d_model = recv.shape
-    n_blk, _, _ = dest_col.shape
-    blk = dest_col.shape[1]
+def low_rows(cap):
+    return cap * 3 // 5 // 8 * 8
+
+
+def moe_kernel(x_hbm, idx_ref, gate_ref, wg_hbm, wu_hbm, wd_hbm, out_hbm, relay_hbm,
+               wg_buf, wu_buf, wd_buf, recv, sendb, back, acc, x_buf, dest, cols,
+               w_recv, w_light, w_heavy, tok_recv, tok_send, ret_recv, ret_send, relay_recv, relay_send, fwd_send,
+               x_sem, out_sem, go_sem, ready_sem):
+    n_src, cap, d_model = back.shape
+    low = low_rows(cap)
+    n_blk, blk, _ = cols.shape
     n_chunk, _, f_chunk = wg_buf.shape
     shard = d_model // NZ
 
@@ -36,7 +41,11 @@
     is_a = c == 0
     inner = jnp.logical_and(z > 0, z < NZ - 1)
     outer = jnp.logical_or(z == 0, z == NZ - 1)
+    is_b = c == 1
     a_inner = jnp.logical_and(is_a, inner)
+    b_inner = jnp.logical_and(is_b, inner)
+    b_outer = jnp.logical_and(is_b, outer)
+    inward = (z + 3) // 3
 
     def plane_id(dx, dy, cc):
         return (x + dx) % 2, (y + dy) % 2, cc
@@ -93,12 +102,12 @@
         @pl.loop(0, n_chunk)
         def _(j):
             for m in range(3):
-                w_copy(j, z, m, False, (z + 3) // 3).start()
+                w_copy(j, z, m, False, inward).start()
 
     def end_wait(j):
         for d in range(1, NZ):
             for m in range(3):
-                w_copy(j, (z + d) % NZ, m, False, (z + 3) // 3).wait_recv()
+                w_copy(j, (z + d) % NZ, m, False, inward).wait_recv()
 
     def sent(j, shards, heavy):
         for s in shards:
@@ -121,18 +130,27 @@
 
         pl.semaphore_signal(go_sem.at[heavy], inc=1, device_id={"expert": p + 1}, device_id_type=MESH)
 
-    def x_load(b, dst):
-        return pltpu.make_async_copy(x_hbm.at[pl.ds(pl.multiple_of(b * blk, blk), blk), :], dst.at[b, pl.ds(0, blk), :], x_sem.at[b])
-
-    @pl.loop(0, n_blk)
-    def _(b):
-        x_load(b, back).start()
+    def x_rows(ref, b):
+        return ref.at[pl.ds(pl.multiple_of(b * blk, blk), blk), :]
+
+    def x_load(b):
+        return pltpu.make_async_copy(x_rows(x_hbm, b), back.at[b, pl.ds(0, blk), :], x_sem.at[b])
+
+    half = blk // 2
+
+    def x_again(b, h):
+        rows = pl.ds(pl.multiple_of(b * blk + h * half, half), half)
+        return pltpu.make_async_copy(x_hbm.at[rows, :], x_buf.at[h], x_sem.at[h])
 
     @pl.loop(0, n_chunk)
     def _(j):
         for m in range(3):
             w_local(j, m).start()
 
+    @pl.loop(0, n_blk)
+    def _(b):
+        x_load(b).start()
+
     barrier = pltpu.get_barrier_semaphore()
     for k in range(1, PEERS):
         dev = plane_dev(*plane_id(k % 2, (k // 2) % 2, (c + k // 4) % 2))
@@ -146,13 +164,13 @@
     def _():
         pl.semaphore_signal(barrier, inc=1, device_id={"data": z + 1}, device_id_type=MESH)
 
-    @pl.when(outer)
-    def _():
-        pl.semaphore_wait(barrier, PEERS)
-
-    @pl.when(inner)
-    def _():
-        pl.semaphore_wait(barrier, PEERS + 1)
+    @pl.when(b_inner)
+    def _():
+        for cc in range(2):
+            dev = {"rep": 1 - x, "data": end, "expert": 2 * (1 - y) + cc}
+            pl.semaphore_signal(barrier, inc=1, device_id=dev, device_id_type=MESH)
+
+    pl.semaphore_wait(barrier, PEERS + 1)
 
     @pl.loop(0, n_chunk)
     def _(j):
@@ -183,17 +201,27 @@
         running = running + jnp.sum(one_hot, axis=1, keepdims=True)
         row = jnp.where(slot < cap, ids.astype(jnp.float32) * cap + slot, -1.0)
         dest[b:b + 1, :] = row.astype(jnp.int32)
-        dest_col[b] = jnp.sum(jnp.where(eye, row, 0.0), axis=1, keepdims=True).astype(jnp.int32)
-        gate_col[b] = jnp.sum(jnp.where(eye, gate_ref[:, b * blk:(b + 1) * blk], 0.0), axis=1, keepdims=True)
+        cols[b, :, 0:1] = jnp.sum(jnp.where(eye, row, 0.0), axis=1, keepdims=True)
+        cols[b, :, 1:2] = jnp.sum(jnp.where(eye, gate_ref[:, b * blk:(b + 1) * blk], 0.0), axis=1, keepdims=True)
 
     @pl.loop(0, n_blk)
     def _(b):
-        x_load(b, back).wait()
+        x_load(b).wait()
 
     def tok_copy(e, dev):
         return pltpu.make_async_remote_copy(
             src_ref=sendb.at[e], dst_ref=recv.at[me], send_sem=tok_send.at[e], recv_sem=tok_recv.at[me],
             device_id=dev, device_id_type=MESH)
+
+    def moved_copy(e):
+        return pltpu.make_async_remote_copy(
+            src_ref=sendb.at[e], dst_ref=recv.at[n_src + c], send_sem=tok_send.at[e], recv_sem=tok_recv.at[n_src + c],
+            device_id={"rep": 1 - x, "data": inward, "expert": 2 * (1 - y) + 1}, device_id_type=MESH)
+
+    def tok_sent():
+        for k in range(1, PEERS):
+            peer = plane_id(k % 2, (k // 2) % 2, (c + k // 4) % 2)
+            tok_copy(plane_num(*peer), plane_dev(*peer)).wait_send()
 
     @pl.loop(0, PEERS)
     def _(k):
@@ -221,7 +249,14 @@
         @pl.when(e != me)
         def _():
             sendb[e] = rows
-            tok_copy(e, plane_dev(*peer)).start()
+
+            @pl.when(jnp.logical_and(outer, k == 6))
+            def _():
+                moved_copy(e).start()
+
+            @pl.when(jnp.logical_or(inner, k != 6))
+            def _():
+                tok_copy(e, plane_dev(*peer)).start()
 
         def at(step):
             return pl.when(jnp.logical_and(a_inner, k == step))
@@ -270,9 +305,18 @@
         dev = plane_dev(*plane_id(k % 2, (k // 2) % 2, (c + k // 4) % 2))
         pl.semaphore_signal(ready_sem, inc=1, device_id=dev, device_id_type=MESH)
 
+    @pl.when(outer)
+    def _():
+        pl.semaphore_signal(ready_sem, inc=1, device_id={"data": inward}, device_id_type=MESH)
+
     @pl.loop(0, n_src)
     def _(s):
         acc[s] = jnp.zeros((cap, d_model), jnp.float32)
+
+    def tok_arrived(s):
+        pltpu.make_async_remote_copy(
+            src_ref=sendb.at[0], dst_ref=recv.at[s], send_sem=tok_send.at[0], recv_sem=tok_recv.at[s],
+            device_id={"data": inward}, device_id_type=MESH).wait_recv()
 
     @pl.when(a_inner)
     def _():
@@ -294,22 +338,27 @@
                 light_own(j)
                 light_end(j)
 
-            pl.semaphore_wait(go_sem.at[1], 1)
-
-            @pl.loop(0, 3)
-            def _(j):
-                heavy_all(j)
-
     for k in range(1, PEERS):
         peer = plane_id(k % 2, (k // 2) % 2, (c + k // 4) % 2)
         s = plane_num(*peer)
-        pltpu.make_async_remote_copy(
-            src_ref=sendb.at[s], dst_ref=recv.at[s], send_sem=tok_send.at[s], recv_sem=tok_recv.at[s],
-            device_id=plane_dev(*peer), device_id_type=MESH).wait_recv()
+
+        @pl.when(jnp.logical_not(b_outer) if k % 4 == 3 else s >= 0)
+        def _():
+            tok_arrived(s)
 
     @pl.when(a_inner)
     def _():
         heavy_mate(5)
+
+    @pl.when(is_b)
+    def _():
+        tok_sent()
+
+    @pl.when(b_inner)
+    def _():
+        for owner in (mate, far):
+            for m in range(3):
+                w_copy(0, owner, m, True, end).wait_recv()
 
     def ffn(j, s):
         rows = recv[s]
@@ -318,6 +367,45 @@
         h = (g * jax.nn.sigmoid(g) * u).astype(jnp.bfloat16)
         return lax.dot_general(h, wd_buf[j], (((1,), (1,)), ((), ())), preferred_element_type=jnp.float32)
 
+    def ret_piece(e, q):
+        return back.at[e, pl.ds(q * low, cap - low if q else low), :]
+
+    def returned(e, qs):
+        @pl.when(e != me)
+        def _():
+            for q in qs:
+                pltpu.make_async_remote_copy(
+                    src_ref=ret_piece(e, q), dst_ref=ret_piece(e, q), send_sem=ret_send.at[e, q], recv_sem=ret_recv.at[e, q],
+                    device_id={"data": inward}, device_id_type=MESH).wait_recv()
+
+    def put_back(b, target, rows):
+        hot = (target.astype(jnp.float32) == cols[b, :, 0:1]).astype(jnp.float32).astype(jnp.bfloat16)
+        return jnp.dot(hot, rows.reshape(target.shape[1], d_model), preferred_element_type=jnp.float32)
+
+    def first_half(k):
+        e = 2 * ((y + k) % 2)
+        for dx in range(2):
+            returned(e + dx, (0, 1))
+        target = lax.broadcasted_iota(jnp.int32, (1, 2 * cap), 1) + e * cap
+
+        @pl.loop(0, n_blk)
+        def _(b):
+            got = put_back(b, target, back[pl.ds(e, 2)])
+            if k == 1:
+                got += sendb[b, 0:blk, :].astype(jnp.float32)
+            sendb[b, 0:blk, :] = got.astype(jnp.bfloat16)
+
+    def last_half(q):
+        rows = cap - low if q else low
+        for e in range(4, 8):
+            returned(e, (q,))
+        col = lax.broadcasted_iota(jnp.int32, (1, 4 * rows), 1)
+        target = (col // rows + 4) * cap + col % rows + q * low
+        return target, slice(q * low, q * low + rows)
+
+    def skipped(s):
+        return jnp.logical_and(b_outer, s % 4 == 2 * (1 - y) + 1 - x)
+
     def before_chunk(j):
         @pl.when(outer)
         def _():
@@ -329,7 +417,16 @@
 
         @pl.loop(0, n_src)
         def _(s):
-            acc[s] += ffn(j, s)
+            @pl.when(jnp.logical_not(skipped(s)))
+            def _():
+                acc[s] += ffn(j, s)
+
+            @pl.when(jnp.logical_and(b_inner, jnp.logical_and(j == 0, s == 3)))
+            def _():
+                pl.semaphore_wait(go_sem.at[1], 1)
+                for owner in (z, mate, far):
+                    pass_on(0, owner, True, False)
+                heavy_all(1)
 
         @pl.when(jnp.logical_and(a_inner, j == 0))
         def _():
@@ -345,85 +442,151 @@
         def _():
             go(sent_heavy, 1)
 
-        @pl.when(jnp.logical_and(jnp.logical_and(c == 1, inner), j < 3))
-        def _():
-            heavy_all(j + 3)
+        @pl.when(jnp.logical_and(b_inner, j < 4))
+        def _():
+            heavy_all(j + 2)
+
+        @pl.when(jnp.logical_and(b_outer, j == 2))
+        def _():
+            first_half(0)
+
+        @pl.when(jnp.logical_and(b_outer, j == 3))
+        def _():
+            first_half(1)
+
+    def relay_copy(i):
+        return pltpu.make_async_remote_copy(
+            src_ref=recv.at[n_src + i], dst_ref=relay_hbm, send_sem=relay_send.at[i], recv_sem=relay_recv,
+            device_id=plane_dev(1 - x, 1 - y, i), device_id_type=MESH)
+
+    @pl.when(b_inner)
+    def _():
+        @pl.loop(0, 2)
+        def _(i):
+            tok_arrived(n_src + i)
+            acc[n_src] = ffn(0, n_src + i)
+
+            @pl.loop(1, n_chunk)
+            def _(j):
+                acc[n_src] += ffn(j, n_src + i)
+
+            recv[n_src + i] = acc[n_src].astype(jnp.bfloat16)
+            relay_copy(i).start()
 
     before_chunk(n_chunk - 1)
-    for k in range(1, PEERS):
-        peer = plane_id(k % 2, (k // 2) % 2, (c + k // 4) % 2)
-        tok_copy(plane_num(*peer), plane_dev(*peer)).wait_send()
-    pl.semaphore_wait(ready_sem, PEERS - 1)
-
-    def ret_copy(s, dev):
+
+    @pl.when(is_a)
+    def _():
+        tok_sent()
+
+    @pl.when(outer)
+    def _():
+        pl.semaphore_wait(ready_sem, PEERS - 1)
+
+    @pl.when(inner)
+    def _():
+        pl.semaphore_wait(ready_sem, PEERS)
+
+    def ret_copy(s, q, dev):
+        piece = pl.ds(q * low, cap - low if q else low)
         return pltpu.make_async_remote_copy(
-            src_ref=sendb.at[s], dst_ref=back.at[me], send_sem=ret_send.at[s], recv_sem=ret_recv.at[me],
+            src_ref=recv.at[s, piece, :], dst_ref=back.at[me, piece, :], send_sem=ret_send.at[s, q], recv_sem=ret_recv.at[me, q],
             device_id=dev, device_id_type=MESH)
+
+    def ret_peer(r):
+        q, rr = r // 4, r % 4
+        return plane_id((1 - q) * ((rr + 1) % 2) + q * (1 - rr // 2), (1 - q) * (rr % 2) + q * (1 - rr // 2), (c + rr // 2 + q * rr) % 2)
+
+    def ret_needed(s):
+        return jnp.logical_and(s != me, jnp.logical_not(skipped(s)))
 
     @pl.loop(0, PEERS)
     def _(r):
-        q, rr = r // 4, r % 4
-        peer = plane_id((1 - q) * ((rr + 1) % 2) + q * (1 - rr // 2), (1 - q) * (rr % 2) + q * (1 - rr // 2), (c + rr // 2 + q * rr) % 2)
+        peer = ret_peer(r)
         s = plane_num(*peer)
-        rows = (acc[s] + ffn(n_chunk - 1, s)).astype(jnp.bfloat16)
-
-        @pl.when(s == me)
-        def _():
-            back[me] = rows
-
-        @pl.when(s != me)
-        def _():
-            sendb[s] = rows
-            ret_copy(s, plane_dev(*peer)).start()
+
+        @pl.when(jnp.logical_not(skipped(s)))
+        def _():
+            rows = (acc[s] + ffn(n_chunk - 1, s)).astype(jnp.bfloat16)
+
+            @pl.when(s == me)
+            def _():
+                back[me] = rows
+
+            @pl.when(s != me)
+            def _():
+                recv[s] = rows
+                ret_copy(s, 0, plane_dev(*peer)).start()
+
+    @pl.loop(0, PEERS)
+    def _(r):
+        peer = ret_peer(r)
+        s = plane_num(*peer)
+
+        @pl.when(ret_needed(s))
+        def _():
+            ret_copy(s, 1, plane_dev(*peer)).start()
+
+    @pl.when(jnp.logical_not(b_outer))
+    def _():
+        first_half(0)
+        first_half(1)
+
+    for h in range(2):
+        x_again(0, h).start()
+
+    target, piece = last_half(0)
 
     @pl.loop(0, n_blk)
     def _(b):
-        x_load(b, recv).start()
+        got = put_back(b, target, back[4:8, piece, :]) + sendb[b, 0:blk, :].astype(jnp.float32)
+        sendb[b, 0:blk, :] = got.astype(jnp.bfloat16)
+
+    def fwd_copy(q):
+        piece = pl.ds(q * low, cap - low if q else low)
+        e = 4 + 2 * (1 - y) + 1 - x
+        return pltpu.make_async_remote_copy(
+            src_ref=relay_hbm.at[piece, :], dst_ref=back.at[e, piece, :], send_sem=fwd_send.at[q], recv_sem=ret_recv.at[e, q],
+            device_id={"data": end}, device_id_type=MESH)
+
+    @pl.when(inner)
+    def _():
+        pltpu.make_async_remote_copy(
+            src_ref=recv.at[0], dst_ref=relay_hbm, send_sem=relay_send.at[0], recv_sem=relay_recv,
+            device_id={"data": mate}, device_id_type=MESH).wait_recv()
+
+        @pl.when(is_b)
+        def _():
+            @pl.loop(0, n_chunk)
+            def _(j):
+                sent_heavy(j)
+
+            pl.semaphore_signal(go_sem.at[2], inc=1, device_id={"expert": p - 1}, device_id_type=MESH)
+
+        @pl.when(is_a)
+        def _():
+            pl.semaphore_wait(go_sem.at[2], 1)
+
+        for q in range(2):
+            fwd_copy(q).start()
+
+    target_hi, piece_hi = last_half(1)
+
+    def out_copy(b):
+        return pltpu.make_async_copy(sendb.at[b, pl.ds(0, blk), :], x_rows(out_hbm, b), out_sem.at[b])
 
     @pl.loop(0, n_blk)
     def _(b):
-        acc[b, 0:blk, :] = jnp.zeros((blk, d_model), jnp.float32)
-
-    def arrived(k):
-        py, pc = (y + k) % 2, k // 2
-        for dx in range(2):
-            peer = ((x + dx) % 2, py, pc)
-            e = plane_num(*peer)
-
-            @pl.when(e != me)
+        mixed = (put_back(b, target_hi, back[4:8, piece_hi, :]) + sendb[b, 0:blk, :].astype(jnp.float32)) * cols[b, :, 1:2]
+        for h in range(2):
+            part = slice(h * half, h * half + half)
+            x_again(b, h).wait()
+            sendb[b, part, :] = (x_buf[h].astype(jnp.float32) + mixed[part]).astype(jnp.bfloat16)
+
+            @pl.when(b + 1 < n_blk)
             def _():
-                pltpu.make_async_remote_copy(
-                    src_ref=sendb.at[e], dst_ref=back.at[e], send_sem=ret_send.at[e], recv_sem=ret_recv.at[e],
-                    device_id=plane_dev(*peer), device_id_type=MESH).wait_recv()
-
-        return 4 * pc + 2 * py
-
-    def put_back(e, b):
-        hot = (lax.broadcasted_iota(jnp.int32, (blk, 2 * cap), 1) + e * cap == dest_col[b]).astype(jnp.float32).astype(jnp.bfloat16)
-        rows = back[pl.ds(e, 2)].reshape(2 * cap, d_model)
-        return jnp.dot(hot, rows, preferred_element_type=jnp.float32)
-
-    @pl.loop(0, PEERS // 2 - 1)
-    def _(k):
-        e = arrived(k)
-
-        @pl.loop(0, n_blk)
-        def _(b):
-            acc[b, 0:blk, :] += put_back(e, b)
-
-    @pl.loop(0, n_blk)
-    def _(b):
-        x_load(b, recv).wait()
-
-    e_last = arrived(PEERS // 2 - 1)
-
-    def out_copy(b):
-        return pltpu.make_async_copy(recv.at[b, pl.ds(0, blk), :], out_hbm.at[pl.ds(pl.multiple_of(b * blk, blk), blk), :], x_sem.at[b])
-
-    @pl.loop(0, n_blk)
-    def _(b):
-        mixed = (acc[b, 0:blk, :] + put_back(e_last, b)) * gate_col[b]
-        recv[b, 0:blk, :] = (recv[b, 0:blk, :].astype(jnp.float32) + mixed).astype(jnp.bfloat16)
+                x_again(b + 1, h).start()
+
         out_copy(b).start()
 
     @pl.loop((n_chunk - 1) * (1 - c), n_chunk)
@@ -435,11 +598,30 @@
         @pl.when(inner)
         def _():
             sent_light(j)
-            sent_heavy(j)
-
-    for k in range(1, PEERS):
-        peer = plane_id(k % 2, (k // 2) % 2, (c + k // 4) % 2)
-        ret_copy(plane_num(*peer), plane_dev(*peer)).wait_send()
+
+    @pl.when(a_inner)
+    def _():
+        sent_heavy(n_chunk - 1)
+
+    @pl.when(b_inner)
+    def _():
+        for i in range(2):
+            relay_copy(i).wait_send()
+
+    @pl.when(inner)
+    def _():
+        for q in range(2):
+            fwd_copy(q).wait_send()
+
+    @pl.loop(0, PEERS)
+    def _(r):
+        peer = ret_peer(r)
+        s = plane_num(*peer)
+
+        @pl.when(ret_needed(s))
+        def _():
+            for q in range(2):
+                ret_copy(s, q, plane_dev(*peer)).wait_send()
 
     @pl.loop(0, n_blk)
     def _(b):
@@ -465,25 +647,25 @@
         dma = pltpu.SemaphoreType.DMA
         return pl.pallas_call(
             moe_kernel,
-            out_shape=jax.ShapeDtypeStruct((tok_rows, d_model), jnp.bfloat16),
+            out_shape=(jax.ShapeDtypeStruct((tok_rows, d_model), jnp.bfloat16), jax.ShapeDtypeStruct((cap, d_model), jnp.bfloat16)),
             in_specs=[any_spec, vmem_spec, vmem_spec, any_spec, any_spec, any_spec],
-            out_specs=any_spec,
+            out_specs=(any_spec, any_spec),
             scratch_shapes=[
                 pltpu.VMEM((CHUNKS, d_model, f_chunk), jnp.bfloat16),
                 pltpu.VMEM((CHUNKS, d_model, f_chunk), jnp.bfloat16),
                 pltpu.VMEM((CHUNKS, d_model, f_chunk), jnp.bfloat16),
+                pltpu.VMEM((PEERS + 2, cap, d_model), jnp.bfloat16),
                 pltpu.VMEM((PEERS, cap, d_model), jnp.bfloat16),
                 pltpu.VMEM((PEERS, cap, d_model), jnp.bfloat16),
-                pltpu.VMEM((PEERS, cap, d_model), jnp.bfloat16),
-                pltpu.VMEM((PEERS, cap, d_model), jnp.float32),
+                pltpu.VMEM((PEERS + 1, cap, d_model), jnp.float32),
+                pltpu.VMEM((2, blk // 2, d_model), jnp.bfloat16),
                 pltpu.VMEM((PEERS, blk), jnp.int32),
-                pltpu.VMEM((PEERS, blk, 1), jnp.int32),
-                pltpu.VMEM((PEERS, blk, 1), jnp.float32),
+                pltpu.VMEM((PEERS, blk, 2), jnp.float32),
                 dma((CHUNKS, NZ, 3)), dma((CHUNKS, NZ, 3)), dma((CHUNKS, NZ, 3)),
-                dma((PEERS,)), dma((PEERS,)), dma((PEERS,)), dma((PEERS,)), dma((PEERS,)),
-                pltpu.SemaphoreType.REGULAR((2,)), pltpu.SemaphoreType.REGULAR,
+                dma((PEERS + 2,)), dma((PEERS,)), dma((PEERS, 2)), dma((PEERS, 2)), dma, dma((2,)), dma((2,)),
+                dma((PEERS,)), dma((PEERS,)), pltpu.SemaphoreType.REGULAR((3,)), pltpu.SemaphoreType.REGULAR,
             ],
             compiler_params=pltpu.CompilerParams(collective_id=0, has_side_effects=True, vmem_limit_bytes=VMEM_BYTES),
-        )(x_loc, idx_loc.T, gate_loc.T, wg_loc, wu_loc, wd_loc.transpose(0, 2, 1))
+        )(x_loc, idx_loc.T, gate_loc.T, wg_loc, wu_loc, wd_loc.transpose(0, 2, 1))[0]
 
     return jax.shard_map(device_step, mesh=mesh, in_specs=(tok_spec, tok_spec, tok_spec, wide_spec, wide_spec, down_spec), out_specs=tok_spec, check_vma=False)

time: 304 us -> 318 us (1.046)
  Pallas kernels: 298 us -> 311 us
    pallas_call x1, Pallas kernels: 298 us -> 311 us  [device_step(): pl.pallas_call(moe_kernel, out_shape=(jax.ShapeDtypeStruct((tok_rows, d_m...]
where the time goes in v4:
time: 318 us; the launch traced here: 317 us
  Pallas kernels  311 us (98%)
  local copies, waits for them, and re-layouts  5.89 us (2%)
    pallas_call x1, Pallas kernels, device_step(): pl.pallas_call(moe_kernel, out_shape=(jax.ShapeDtypeStruct((tok_rows, d_m...  311 us

profile of v4, /device:TPU:0, one launch (start us, length us, event | category | flops | bytes accessed | tf_op | source)
XLA Modules:
  0.0 317.3 jit_solution(1424158377200044987)
XLA Ops:
  0.0 311.4 %shard_map.64 = (bf16[4096,768]{1,0:T(8,128)(2,1)}, bf16[640,768]{1,0:T(8,128)(2,1)}) custom-call(bf16[4096,768]{1,0:T(8,128)(2,1)} %x_hbm.1, s32[1,4096]{1,0:T(1,128)} %bitcast.4, f32[1,4096]{1,0:T(1,128)} %bitcast.5, bf16[2,192,3072]{2,1,0:T(8,128)(2,1)} %wg_hbm.1, bf16[2,192,3072]{2,1,0:T(8,128)(2,1)} %wu_hbm.1, bf16[2,192,3072]{2,1,0:T(8,128)(2,1)} %bitcast.3), custom_call_target="tpu_custom_call" | custom-call | tf_op jit(solution)/shard_map/pallas_call | solution.py:648
  311.4 5.9 %copy.8 = bf16[4096,768]{1,0:T(8,128)(2,1)} copy(bf16[4096,768]{1,0:T(8,128)(2,1)} %get-tuple-element.6) | data formatting | bytes 12582912

commit v5 on v4

--- a/solution.py
+++ b/solution.py
@@ -164,13 +164,13 @@
     def _():
         pl.semaphore_signal(barrier, inc=1, device_id={"data": z + 1}, device_id_type=MESH)
 
-    @pl.when(b_inner)
-    def _():
-        for cc in range(2):
-            dev = {"rep": 1 - x, "data": end, "expert": 2 * (1 - y) + cc}
-            pl.semaphore_signal(barrier, inc=1, device_id=dev, device_id_type=MESH)
-
-    pl.semaphore_wait(barrier, PEERS + 1)
+    @pl.when(outer)
+    def _():
+        pl.semaphore_wait(barrier, PEERS)
+
+    @pl.when(inner)
+    def _():
+        pl.semaphore_wait(barrier, PEERS + 1)
 
     @pl.loop(0, n_chunk)
     def _(j):
@@ -213,11 +213,6 @@
             src_ref=sendb.at[e], dst_ref=recv.at[me], send_sem=tok_send.at[e], recv_sem=tok_recv.at[me],
             device_id=dev, device_id_type=MESH)
 
-    def moved_copy(e):
-        return pltpu.make_async_remote_copy(
-            src_ref=sendb.at[e], dst_ref=recv.at[n_src + c], send_sem=tok_send.at[e], recv_sem=tok_recv.at[n_src + c],
-            device_id={"rep": 1 - x, "data": inward, "expert": 2 * (1 - y) + 1}, device_id_type=MESH)
-
     def tok_sent():
         for k in range(1, PEERS):
             peer = plane_id(k % 2, (k // 2) % 2, (c + k // 4) % 2)
@@ -250,13 +245,7 @@
         def _():
             sendb[e] = rows
 
-            @pl.when(jnp.logical_and(outer, k == 6))
-            def _():
-                moved_copy(e).start()
-
-            @pl.when(jnp.logical_or(inner, k != 6))
-            def _():
-                tok_copy(e, plane_dev(*peer)).start()
+            tok_copy(e, plane_dev(*peer)).start()
 
         def at(step):
             return pl.when(jnp.logical_and(a_inner, k == step))
@@ -341,10 +330,17 @@
     for k in range(1, PEERS):
         peer = plane_id(k % 2, (k // 2) % 2, (c + k // 4) % 2)
         s = plane_num(*peer)
-
-        @pl.when(jnp.logical_not(b_outer) if k % 4 == 3 else s >= 0)
-        def _():
-            tok_arrived(s)
+        tok_arrived(s)
+
+    def moved_copy(i):
+        return pltpu.make_async_remote_copy(
+            src_ref=recv.at[plane_num(1 - x, 1 - y, i)], dst_ref=recv.at[n_src + i], send_sem=relay_send.at[i],
+            recv_sem=tok_recv.at[n_src + i], device_id={"data": inward}, device_id_type=MESH)
+
+    @pl.when(b_outer)
+    def _():
+        for i in range(2):
+            moved_copy(i).start()
 
     @pl.when(a_inner)
     def _():
@@ -527,21 +523,6 @@
         def _():
             ret_copy(s, 1, plane_dev(*peer)).start()
 
-    @pl.when(jnp.logical_not(b_outer))
-    def _():
-        first_half(0)
-        first_half(1)
-
-    for h in range(2):
-        x_again(0, h).start()
-
-    target, piece = last_half(0)
-
-    @pl.loop(0, n_blk)
-    def _(b):
-        got = put_back(b, target, back[4:8, piece, :]) + sendb[b, 0:blk, :].astype(jnp.float32)
-        sendb[b, 0:blk, :] = got.astype(jnp.bfloat16)
-
     def fwd_copy(q):
         piece = pl.ds(q * low, cap - low if q else low)
         e = 4 + 2 * (1 - y) + 1 - x
@@ -549,8 +530,7 @@
             src_ref=relay_hbm.at[piece, :], dst_ref=back.at[e, piece, :], send_sem=fwd_send.at[q], recv_sem=ret_recv.at[e, q],
             device_id={"data": end}, device_id_type=MESH)
 
-    @pl.when(inner)
-    def _():
+    def relay():
         pltpu.make_async_remote_copy(
             src_ref=recv.at[0], dst_ref=relay_hbm, send_sem=relay_send.at[0], recv_sem=relay_recv,
             device_id={"data": mate}, device_id_type=MESH).wait_recv()
@@ -569,6 +549,30 @@
 
         for q in range(2):
             fwd_copy(q).start()
+
+    @pl.when(jnp.logical_not(b_outer))
+    def _():
+        first_half(0)
+
+        @pl.when(b_inner)
+        def _():
+            relay()
+
+        first_half(1)
+
+        @pl.when(a_inner)
+        def _():
+            relay()
+
+    for h in range(2):
+        x_again(0, h).start()
+
+    target, piece = last_half(0)
+
+    @pl.loop(0, n_blk)
+    def _(b):
+        got = put_back(b, target, back[4:8, piece, :]) + sendb[b, 0:blk, :].astype(jnp.float32)
+        sendb[b, 0:blk, :] = got.astype(jnp.bfloat16)
 
     target_hi, piece_hi = last_half(1)
 
@@ -607,6 +611,11 @@
     def _():
         for i in range(2):
             relay_copy(i).wait_send()
+
+    @pl.when(b_outer)
+    def _():
+        for i in range(2):
+            moved_copy(i).wait_send()
 
     @pl.when(inner)
     def _():

time: 318 us -> 285 us (0.90)
  Pallas kernels: 311 us -> 279 us
    pallas_call x1, Pallas kernels: 311 us -> 279 us  [device_step(): pl.pallas_call(moe_kernel, out_shape=(jax.ShapeDtypeStruct((tok_rows, d_m...]
where the time goes in v5:
time: 285 us
  Pallas kernels  279 us (98%)
  local copies, waits for them, and re-layouts  5.89 us (2%)
    pallas_call x1, Pallas kernels, device_step(): pl.pallas_call(moe_kernel, out_shape=(jax.ShapeDtypeStruct((tok_rows, d_m...  279 us
    unnamed x1, local copies, waits for them, and re-layouts  5.89 us

profile of v5, /device:TPU:0, one launch (start us, length us, event | category | flops | bytes accessed | tf_op | source)
XLA Modules:
  0.0 284.7 jit_solution(3225225185141818395)
XLA Ops:
  0.0 278.8 %shard_map.64 = (bf16[4096,768]{1,0:T(8,128)(2,1)}, bf16[640,768]{1,0:T(8,128)(2,1)}) custom-call(bf16[4096,768]{1,0:T(8,128)(2,1)} %x_hbm.1, s32[1,4096]{1,0:T(1,128)} %bitcast.4, f32[1,4096]{1,0:T(1,128)} %bitcast.5, bf16[2,192,3072]{2,1,0:T(8,128)(2,1)} %wg_hbm.1, bf16[2,192,3072]{2,1,0:T(8,128)(2,1)} %wu_hbm.1, bf16[2,192,3072]{2,1,0:T(8,128)(2,1)} %bitcast.3), custom_call_target="tpu_custom_call" | custom-call | tf_op jit(solution)/shard_map/pallas_call | solution.py:657
  278.8 5.9 %copy.8 = bf16[4096,768]{1,0:T(8,128)(2,1)} copy(bf16[4096,768]{1,0:T(8,128)(2,1)} %get-tuple-element.6) | data formatting | bytes 12582912

commit v6 on v5

--- a/solution.py
+++ b/solution.py
@@ -19,8 +19,8 @@
     return max(8, ((5 * top_k * tok_rows) // (4 * n_exp) + 7) // 8 * 8)
 
 
-def low_rows(cap):
-    return cap * 3 // 5 // 8 * 8
+def slot_edges(cap):
+    return 0, cap * 2 // 5, cap * 4 // 5, cap
 
 
 def moe_kernel(x_hbm, idx_ref, gate_ref, wg_hbm, wu_hbm, wd_hbm, out_hbm, relay_hbm,
@@ -28,7 +28,8 @@
                w_recv, w_light, w_heavy, tok_recv, tok_send, ret_recv, ret_send, relay_recv, relay_send, fwd_send,
                x_sem, out_sem, go_sem, ready_sem):
     n_src, cap, d_model = back.shape
-    low = low_rows(cap)
+    edges = slot_edges(cap)
+    pieces = range(len(edges) - 1)
     n_blk, blk, _ = cols.shape
     n_chunk, _, f_chunk = wg_buf.shape
     shard = d_model // NZ
@@ -363,16 +364,16 @@
         h = (g * jax.nn.sigmoid(g) * u).astype(jnp.bfloat16)
         return lax.dot_general(h, wd_buf[j], (((1,), (1,)), ((), ())), preferred_element_type=jnp.float32)
 
-    def ret_piece(e, q):
-        return back.at[e, pl.ds(q * low, cap - low if q else low), :]
-
-    def returned(e, qs):
-        @pl.when(e != me)
+    def piece_of(ref, e, q):
+        return ref.at[e, pl.ds(edges[q], edges[q + 1] - edges[q]), :]
+
+    def returned(e, qs, wanted):
+        @pl.when(wanted)
         def _():
             for q in qs:
                 pltpu.make_async_remote_copy(
-                    src_ref=ret_piece(e, q), dst_ref=ret_piece(e, q), send_sem=ret_send.at[e, q], recv_sem=ret_recv.at[e, q],
-                    device_id={"data": inward}, device_id_type=MESH).wait_recv()
+                    src_ref=piece_of(back, e, q), dst_ref=piece_of(back, e, q), send_sem=ret_send.at[e, q],
+                    recv_sem=ret_recv.at[e, q], device_id={"data": inward}, device_id_type=MESH).wait_recv()
 
     def put_back(b, target, rows):
         hot = (target.astype(jnp.float32) == cols[b, :, 0:1]).astype(jnp.float32).astype(jnp.bfloat16)
@@ -381,7 +382,7 @@
     def first_half(k):
         e = 2 * ((y + k) % 2)
         for dx in range(2):
-            returned(e + dx, (0, 1))
+            returned(e + dx, pieces, e + dx != me)
         target = lax.broadcasted_iota(jnp.int32, (1, 2 * cap), 1) + e * cap
 
         @pl.loop(0, n_blk)
@@ -391,13 +392,23 @@
                 got += sendb[b, 0:blk, :].astype(jnp.float32)
             sendb[b, 0:blk, :] = got.astype(jnp.bfloat16)
 
-    def last_half(q):
-        rows = cap - low if q else low
-        for e in range(4, 8):
-            returned(e, (q,))
-        col = lax.broadcasted_iota(jnp.int32, (1, 4 * rows), 1)
-        target = (col // rows + 4) * cap + col % rows + q * low
-        return target, slice(q * low, q * low + rows)
+    def own_chip():
+        returned(4, pieces, is_a)
+        target = lax.broadcasted_iota(jnp.int32, (1, cap), 1) + (4 + 2 * y + x) * cap
+
+        @pl.loop(0, n_blk)
+        def _(b):
+            got = put_back(b, target, back[4]) + sendb[b, 0:blk, :].astype(jnp.float32)
+            sendb[b, 0:blk, :] = got.astype(jnp.bfloat16)
+
+    def others(q):
+        rows = edges[q + 1] - edges[q]
+        for e in range(5, 8):
+            returned(e, (q,), p >= 0)
+        col = lax.broadcasted_iota(jnp.int32, (1, 3 * rows), 1)
+        i = col // rows
+        expert = 4 + 2 * ((y + (i + 1) // 2) % 2) + (x + 1 - i % 2) % 2
+        return expert * cap + edges[q] + col % rows, slice(edges[q], edges[q + 1])
 
     def skipped(s):
         return jnp.logical_and(b_outer, s % 4 == 2 * (1 - y) + 1 - x)
@@ -483,11 +494,14 @@
     def _():
         pl.semaphore_wait(ready_sem, PEERS)
 
-    def ret_copy(s, q, dev):
-        piece = pl.ds(q * low, cap - low if q else low)
+    def back_slot(peer):
+        return (1 - c) * me + c * (4 + (x + peer[0]) % 2 + 2 * ((y + peer[1]) % 2))
+
+    def ret_copy(peer, q):
+        d = back_slot(peer)
         return pltpu.make_async_remote_copy(
-            src_ref=recv.at[s, piece, :], dst_ref=back.at[me, piece, :], send_sem=ret_send.at[s, q], recv_sem=ret_recv.at[me, q],
-            device_id=dev, device_id_type=MESH)
+            src_ref=piece_of(recv, plane_num(*peer), q), dst_ref=piece_of(back, d, q), send_sem=ret_send.at[plane_num(*peer), q],
+            recv_sem=ret_recv.at[d, q], device_id=plane_dev(*peer), device_id_type=MESH)
 
     def ret_peer(r):
         q, rr = r // 4, r % 4
@@ -507,12 +521,124 @@
 
             @pl.when(s == me)
             def _():
-                back[me] = rows
+                back[back_slot(peer)] = rows
 
             @pl.when(s != me)
             def _():
                 recv[s] = rows
-                ret_copy(s, 0, plane_dev(*peer)).start()
+                ret_copy(peer, 0).start()
+
+    for q in pieces[1:]:
+        @pl.loop(0, PEERS)
+        def _(r):
+            peer = ret_peer(r)
+
+            @pl.when(ret_needed(plane_num(*peer)))
+            def _():
+                ret_copy(peer, q).start()
+
+    def fwd_copy(q):
+        return pltpu.make_async_remote_copy(
+            src_ref=relay_hbm.at[pl.ds(edges[q], edges[q + 1] - edges[q]), :], dst_ref=piece_of(back, 7, q), send_sem=fwd_send.at[q],
+            recv_sem=ret_recv.at[7, q], device_id={"data": end}, device_id_type=MESH)
+
+    def relay():
+        pltpu.make_async_remote_copy(
+            src_ref=recv.at[0], dst_ref=relay_hbm, send_sem=relay_send.at[0], recv_sem=relay_recv,
+            device_id={"data": mate}, device_id_type=MESH).wait_recv()
+
+        @pl.when(is_b)
+        def _():
+            @pl.loop(0, n_chunk)
+            def _(j):
+                sent_heavy(j)
+
+            pl.semaphore_signal(go_sem.at[2], inc=1, device_id={"expert": p - 1}, device_id_type=MESH)
+
+        @pl.when(is_a)
+        def _():
+            pl.semaphore_wait(go_sem.at[2], 1)
+
+        for q in pieces:
+            fwd_copy(q).start()
+
+    @pl.when(jnp.logical_not(b_outer))
+    def _():
+        first_half(0)
+
+        @pl.when(b_inner)
+        def _():
+            relay()
+
+        first_half(1)
+
+        @pl.when(a_inner)
+        def _():
+            relay()
+
+    for h in range(2):
+        x_again(0, h).start()
+
+    own_chip()
+
+    def middle(q):
+        target, piece = others(q)
+
+        @pl.loop(0, n_blk)
+        def _(b):
+            got = put_back(b, target, back[5:8, piece, :]) + sendb[b, 0:blk, :].astype(jnp.float32)
+            sendb[b, 0:blk, :] = got.astype(jnp.bfloat16)
+
+    for q in pieces[:-1]:
+        middle(q)
+
+    target, piece = others(pieces[-1])
+
+    def out_copy(b):
+        return pltpu.make_async_copy(sendb.at[b, pl.ds(0, blk), :], x_rows(out_hbm, b), out_sem.at[b])
+
+    @pl.loop(0, n_blk)
+    def _(b):
+        mixed = (put_back(b, target, back[5:8, piece, :]) + sendb[b, 0:blk, :].astype(jnp.float32)) * cols[b, :, 1:2]
+        for h in range(2):
+            part = slice(h * half, h * half + half)
+            x_again(b, h).wait()
+            sendb[b, part, :] = (x_buf[h].astype(jnp.float32) + mixed[part]).astype(jnp.bfloat16)
+
+            @pl.when(b + 1 < n_blk)
+            def _():
+                x_again(b + 1, h).start()
+
+        out_copy(b).start()
+
+    @pl.loop((n_chunk - 1) * (1 - c), n_chunk)
+    def _(j):
+        @pl.when(outer)
+        def _():
+            sent_outer(j)
+
+        @pl.when(inner)
+        def _():
+            sent_light(j)
+
+    @pl.when(a_inner)
+    def _():
+        sent_heavy(n_chunk - 1)
+
+    @pl.when(b_inner)
+    def _():
+        for i in range(2):
+            relay_copy(i).wait_send()
+
+    @pl.when(b_outer)
+    def _():
+        for i in range(2):
+            moved_copy(i).wait_send()
+
+    @pl.when(inner)
+    def _():
+        for q in pieces:
+            fwd_copy(q).wait_send()
 
     @pl.loop(0, PEERS)
     def _(r):
@@ -521,116 +647,8 @@
 
         @pl.when(ret_needed(s))
         def _():
-            ret_copy(s, 1, plane_dev(*peer)).start()
-
-    def fwd_copy(q):
-        piece = pl.ds(q * low, cap - low if q else low)
-        e = 4 + 2 * (1 - y) + 1 - x
-        return pltpu.make_async_remote_copy(
-            src_ref=relay_hbm.at[piece, :], dst_ref=back.at[e, piece, :], send_sem=fwd_send.at[q], recv_sem=ret_recv.at[e, q],
-            device_id={"data": end}, device_id_type=MESH)
-
-    def relay():
-        pltpu.make_async_remote_copy(
-            src_ref=recv.at[0], dst_ref=relay_hbm, send_sem=relay_send.at[0], recv_sem=relay_recv,
-            device_id={"data": mate}, device_id_type=MESH).wait_recv()
-
-        @pl.when(is_b)
-        def _():
-            @pl.loop(0, n_chunk)
-            def _(j):
-                sent_heavy(j)
-
-            pl.semaphore_signal(go_sem.at[2], inc=1, device_id={"expert": p - 1}, device_id_type=MESH)
-
-        @pl.when(is_a)
-        def _():
-            pl.semaphore_wait(go_sem.at[2], 1)
-
-        for q in range(2):
-            fwd_copy(q).start()
-
-    @pl.when(jnp.logical_not(b_outer))
-    def _():
-        first_half(0)
-
-        @pl.when(b_inner)
-        def _():
-            relay()
-
-        first_half(1)
-
-        @pl.when(a_inner)
-        def _():
-            relay()
-
-    for h in range(2):
-        x_again(0, h).start()
-
-    target, piece = last_half(0)
-
-    @pl.loop(0, n_blk)
-    def _(b):
-        got = put_back(b, target, back[4:8, piece, :]) + sendb[b, 0:blk, :].astype(jnp.float32)
-        sendb[b, 0:blk, :] = got.astype(jnp.bfloat16)
-
-    target_hi, piece_hi = last_half(1)
-
-    def out_copy(b):
-        return pltpu.make_async_copy(sendb.at[b, pl.ds(0, blk), :], x_rows(out_hbm, b), out_sem.at[b])
-
-    @pl.loop(0, n_blk)
-    def _(b):
-        mixed = (put_back(b, target_hi, back[4:8, piece_hi, :]) + sendb[b, 0:blk, :].astype(jnp.float32)) * cols[b, :, 1:2]
-        for h in range(2):
-            part = slice(h * half, h * half + half)
-            x_again(b, h).wait()
-            sendb[b, part, :] = (x_buf[h].astype(jnp.float32) + mixed[part]).astype(jnp.bfloat16)
-
-            @pl.when(b + 1 < n_blk)
-            def _():
-                x_again(b + 1, h).start()
-
-        out_copy(b).start()
-
-    @pl.loop((n_chunk - 1) * (1 - c), n_chunk)
-    def _(j):
-        @pl.when(outer)
-        def _():
-            sent_outer(j)
-
-        @pl.when(inner)
-        def _():
-            sent_light(j)
-
-    @pl.when(a_inner)
-    def _():
-        sent_heavy(n_chunk - 1)
-
-    @pl.when(b_inner)
-    def _():
-        for i in range(2):
-            relay_copy(i).wait_send()
-
-    @pl.when(b_outer)
-    def _():
-        for i in range(2):
-            moved_copy(i).wait_send()
-
-    @pl.when(inner)
-    def _():
-        for q in range(2):
-            fwd_copy(q).wait_send()
-
-    @pl.loop(0, PEERS)
-    def _(r):
-        peer = ret_peer(r)
-        s = plane_num(*peer)
-
-        @pl.when(ret_needed(s))
-        def _():
-            for q in range(2):
-                ret_copy(s, q, plane_dev(*peer)).wait_send()
+            for q in pieces:
+                ret_copy(peer, q).wait_send()
 
     @pl.loop(0, n_blk)
     def _(b):
@@ -671,7 +689,7 @@
                 pltpu.VMEM((PEERS, blk), jnp.int32),
                 pltpu.VMEM((PEERS, blk, 2), jnp.float32),
                 dma((CHUNKS, NZ, 3)), dma((CHUNKS, NZ, 3)), dma((CHUNKS, NZ, 3)),
-                dma((PEERS + 2,)), dma((PEERS,)), dma((PEERS, 2)), dma((PEERS, 2)), dma, dma((2,)), dma((2,)),
+                dma((PEERS + 2,)), dma((PEERS,)), dma((PEERS, 3)), dma((PEERS, 3)), dma, dma((2,)), dma((3,)),
                 dma((PEERS,)), dma((PEERS,)), pltpu.SemaphoreType.REGULAR((3,)), pltpu.SemaphoreType.REGULAR,
             ],
             compiler_params=pltpu.CompilerParams(collective_id=0, has_side_effects=True, vmem_limit_bytes=VMEM_BYTES),

time: 285 us -> 288 us (1.011)
  Pallas kernels: 279 us -> 282 us
    pallas_call x1, Pallas kernels: 279 us -> 282 us  [device_step(): pl.pallas_call(moe_kernel, out_shape=(jax.ShapeDtypeStruct((tok_rows, d_m...]
where the time goes in v6:
time: 288 us
  Pallas kernels  282 us (98%)
  local copies, waits for them, and re-layouts  5.89 us (2%)
    pallas_call x1, Pallas kernels, device_step(): pl.pallas_call(moe_kernel, out_shape=(jax.ShapeDtypeStruct((tok_rows, d_m...  282 us
    unnamed x1, local copies, waits for them, and re-layouts  5.89 us

profile of v6, /device:TPU:0, one launch (start us, length us, event | category | flops | bytes accessed | tf_op | source)
XLA Modules:
  0.0 287.8 jit_solution(4342400773713249477)
XLA Ops:
  0.0 281.9 %shard_map.64 = (bf16[4096,768]{1,0:T(8,128)(2,1)}, bf16[640,768]{1,0:T(8,128)(2,1)}) custom-call(bf16[4096,768]{1,0:T(8,128)(2,1)} %x_hbm.1, s32[1,4096]{1,0:T(1,128)} %bitcast.4, f32[1,4096]{1,0:T(1,128)} %bitcast.5, bf16[2,192,3072]{2,1,0:T(8,128)(2,1)} %wg_hbm.1, bf16[2,192,3072]{2,1,0:T(8,128)(2,1)} %wu_hbm.1, bf16[2,192,3072]{2,1,0:T(8,128)(2,1)} %bitcast.3), custom_call_target="tpu_custom_call" | custom-call | tf_op jit(solution)/shard_map/pallas_call | solution.py:675
  281.9 5.9 %copy.8 = bf16[4096,768]{1,0:T(8,128)(2,1)} copy(bf16[4096,768]{1,0:T(8,128)(2,1)} %get-tuple-element.6) | data formatting | bytes 12582912

commit v7 on v6

--- a/solution.py
+++ b/solution.py
@@ -20,11 +20,11 @@
 
 
 def slot_edges(cap):
-    return 0, cap * 2 // 5, cap * 4 // 5, cap
+    return 0, cap * 3 // 5, cap
 
 
 def moe_kernel(x_hbm, idx_ref, gate_ref, wg_hbm, wu_hbm, wd_hbm, out_hbm, relay_hbm,
-               wg_buf, wu_buf, wd_buf, recv, sendb, back, acc, x_buf, dest, cols,
+               wg_buf, wu_buf, wd_buf, recv, sendb, back, acc, dest, cols,
                w_recv, w_light, w_heavy, tok_recv, tok_send, ret_recv, ret_send, relay_recv, relay_send, fwd_send,
                x_sem, out_sem, go_sem, ready_sem):
     n_src, cap, d_model = back.shape
@@ -137,11 +137,8 @@
     def x_load(b):
         return pltpu.make_async_copy(x_rows(x_hbm, b), back.at[b, pl.ds(0, blk), :], x_sem.at[b])
 
-    half = blk // 2
-
-    def x_again(b, h):
-        rows = pl.ds(pl.multiple_of(b * blk + h * half, half), half)
-        return pltpu.make_async_copy(x_hbm.at[rows, :], x_buf.at[h], x_sem.at[h])
+    def x_again(b):
+        return pltpu.make_async_copy(x_rows(x_hbm, b), back.at[b % 4, pl.ds(0, blk), :], x_sem.at[b % 4])
 
     @pl.loop(0, n_chunk)
     def _(j):
@@ -504,6 +501,8 @@
             recv_sem=ret_recv.at[d, q], device_id=plane_dev(*peer), device_id_type=MESH)
 
     def ret_peer(r):
+        third = (r + 5) // 8
+        r = r + 4 * ((r + 6) // 8 - third) - third + (r + 1) // 8
         q, rr = r // 4, r % 4
         return plane_id((1 - q) * ((rr + 1) % 2) + q * (1 - rr // 2), (1 - q) * (rr % 2) + q * (1 - rr // 2), (c + rr // 2 + q * rr) % 2)
 
@@ -576,8 +575,8 @@
         def _():
             relay()
 
-    for h in range(2):
-        x_again(0, h).start()
+    for b in range(4):
+        x_again(b).start()
 
     own_chip()
 
@@ -600,14 +599,12 @@
     @pl.loop(0, n_blk)
     def _(b):
         mixed = (put_back(b, target, back[5:8, piece, :]) + sendb[b, 0:blk, :].astype(jnp.float32)) * cols[b, :, 1:2]
-        for h in range(2):
-            part = slice(h * half, h * half + half)
-            x_again(b, h).wait()
-            sendb[b, part, :] = (x_buf[h].astype(jnp.float32) + mixed[part]).astype(jnp.bfloat16)
-
-            @pl.when(b + 1 < n_blk)
-            def _():
-                x_again(b + 1, h).start()
+        x_again(b).wait()
+        sendb[b, 0:blk, :] = (back[b % 4, 0:blk, :].astype(jnp.float32) + mixed).astype(jnp.bfloat16)
+
+        @pl.when(b + 4 < n_blk)
+        def _():
+            x_again(b + 4).start()
 
         out_copy(b).start()
 
@@ -685,11 +682,10 @@
                 pltpu.VMEM((PEERS, cap, d_model), jnp.bfloat16),
                 pltpu.VMEM((PEERS, cap, d_model), jnp.bfloat16),
                 pltpu.VMEM((PEERS + 1, cap, d_model), jnp.float32),
-                pltpu.VMEM((2, blk // 2, d_model), jnp.bfloat16),
                 pltpu.VMEM((PEERS, blk), jnp.int32),
                 pltpu.VMEM((PEERS, blk, 2), jnp.float32),
                 dma((CHUNKS, NZ, 3)), dma((CHUNKS, NZ, 3)), dma((CHUNKS, NZ, 3)),
-                dma((PEERS + 2,)), dma((PEERS,)), dma((PEERS, 3)), dma((PEERS, 3)), dma, dma((2,)), dma((3,)),
+                dma((PEERS + 2,)), dma((PEERS,)), dma((PEERS, 2)), dma((PEERS, 2)), dma, dma((2,)), dma((2,)),
                 dma((PEERS,)), dma((PEERS,)), pltpu.SemaphoreType.REGULAR((3,)), pltpu.SemaphoreType.REGULAR,
             ],
             compiler_params=pltpu.CompilerParams(collective_id=0, has_side_effects=True, vmem_limit_bytes=VMEM_BYTES),

time: 288 us -> 283 us (0.983)
  Pallas kernels: 282 us -> 277 us
    pallas_call x1, Pallas kernels: 282 us -> 277 us  [device_step(): pl.pallas_call(moe_kernel, out_shape=(jax.ShapeDtypeStruct((tok_rows, d_m...]
where the time goes in v7:
time: 283 us
  Pallas kernels  277 us (98%)
  local copies, waits for them, and re-layouts  5.89 us (2%)
    pallas_call x1, Pallas kernels, device_step(): pl.pallas_call(moe_kernel, out_shape=(jax.ShapeDtypeStruct((tok_rows, d_m...  277 us
    unnamed x1, local copies, waits for them, and re-layouts  5.89 us

profile of v7, /device:TPU:0, one launch (start us, length us, event | category | flops | bytes accessed | tf_op | source)
XLA Modules:
  0.0 282.6 jit_solution(7701099483877317291)
XLA Ops:
  0.0 276.7 %shard_map.64 = (bf16[4096,768]{1,0:T(8,128)(2,1)}, bf16[640,768]{1,0:T(8,128)(2,1)}) custom-call(bf16[4096,768]{1,0:T(8,128)(2,1)} %x_hbm.1, s32[1,4096]{1,0:T(1,128)} %bitcast.4, f32[1,4096]{1,0:T(1,128)} %bitcast.5, bf16[2,192,3072]{2,1,0:T(8,128)(2,1)} %wg_hbm.1, bf16[2,192,3072]{2,1,0:T(8,128)(2,1)} %wu_hbm.1, bf16[2,192,3072]{2,1,0:T(8,128)(2,1)} %bitcast.3), custom_call_target="tpu_custom_call" | custom-call | tf_op jit(solution)/shard_map/pallas_call | solution.py:672
  276.7 5.9 %copy.8 = bf16[4096,768]{1,0:T(8,128)(2,1)} copy(bf16[4096,768]{1,0:T(8,128)(2,1)} %get-tuple-element.6) | data formatting | bytes 12582912

commit v8 on v7

--- a/solution.py
+++ b/solution.py
@@ -64,35 +64,35 @@
         src = (wg_hbm, wu_hbm, wd_hbm)[m].at[x, :, pl.ds(pl.multiple_of(j * f_chunk, f_chunk), f_chunk)]
         return pltpu.make_async_copy(src, w_view(j, z, m), w_recv.at[j, z, m])
 
-    def w_copy(j, s, m, heavy, dev):
+    def w_copy(j, s, m, heavy, dev, role=0):
         view = w_view(j, s, m)
         return pltpu.make_async_remote_copy(
-            src_ref=view, dst_ref=view, send_sem=(w_heavy if heavy else w_light).at[j, s, m], recv_sem=w_recv.at[j, s, m],
+            src_ref=view, dst_ref=view, send_sem=(w_heavy if heavy else w_light).at[j, role], recv_sem=w_recv.at[j, s, m],
             device_id={"data": dev}, device_id_type=MESH)
 
     end, far, mate = 3 * (z - 1), 3 * (2 - z), 3 - z
 
-    def pass_on(j, s, heavy, arrives=True):
+    def pass_on(j, s, heavy, role, arrives=True):
         for m in range(3):
-            cp = w_copy(j, s, m, heavy, end if heavy else mate)
+            cp = w_copy(j, s, m, heavy, end if heavy else mate, role)
             if arrives:
                 cp.wait_recv()
             cp.start()
 
     def light_own(j):
-        pass_on(j, z, False, False)
+        pass_on(j, z, False, 0, False)
 
     def light_end(j):
-        pass_on(j, end, False)
+        pass_on(j, end, False, 1)
 
     def heavy_own(j):
-        pass_on(j, z, True, False)
+        pass_on(j, z, True, 0, False)
 
     def heavy_mate(j):
-        pass_on(j, mate, True)
+        pass_on(j, mate, True, 1)
 
     def heavy_far(j):
-        pass_on(j, far, True)
+        pass_on(j, far, True, 2)
 
     def heavy_all(j):
         heavy_own(j)
@@ -110,19 +110,21 @@
             for m in range(3):
                 w_copy(j, (z + d) % NZ, m, False, inward).wait_recv()
 
-    def sent(j, shards, heavy):
-        for s in shards:
-            for m in range(3):
-                w_copy(j, s, m, heavy, (z + 1) % NZ).wait_send()
+    def sent(j, roles, heavy):
+        rows = wg_buf.at[j, pl.ds(0, 3 * shard), :]
+        for role in range(roles):
+            pltpu.make_async_remote_copy(
+                src_ref=rows, dst_ref=rows, send_sem=(w_heavy if heavy else w_light).at[j, role], recv_sem=w_recv.at[j, 0, 0],
+                device_id={"data": inward}, device_id_type=MESH).wait_send()
 
     def sent_outer(j):
-        sent(j, (z,), False)
+        sent(j, 1, False)
 
     def sent_light(j):
-        sent(j, (z, end), False)
+        sent(j, 2, False)
 
     def sent_heavy(j):
-        sent(j, (z, mate, far), True)
+        sent(j, 3, True)
 
     def go(done, heavy):
         @pl.loop(0, n_chunk - 1)
@@ -428,8 +430,8 @@
             @pl.when(jnp.logical_and(b_inner, jnp.logical_and(j == 0, s == 3)))
             def _():
                 pl.semaphore_wait(go_sem.at[1], 1)
-                for owner in (z, mate, far):
-                    pass_on(0, owner, True, False)
+                for role, owner in enumerate((z, mate, far)):
+                    pass_on(0, owner, True, role, False)
                 heavy_all(1)
 
         @pl.when(jnp.logical_and(a_inner, j == 0))
@@ -684,7 +686,7 @@
                 pltpu.VMEM((PEERS + 1, cap, d_model), jnp.float32),
                 pltpu.VMEM((PEERS, blk), jnp.int32),
                 pltpu.VMEM((PEERS, blk, 2), jnp.float32),
-                dma((CHUNKS, NZ, 3)), dma((CHUNKS, NZ, 3)), dma((CHUNKS, NZ, 3)),
+                dma((CHUNKS, NZ, 3)), dma((CHUNKS, 2)), dma((CHUNKS, 3)),
                 dma((PEERS + 2,)), dma((PEERS,)), dma((PEERS, 2)), dma((PEERS, 2)), dma, dma((2,)), dma((2,)),
                 dma((PEERS,)), dma((PEERS,)), pltpu.SemaphoreType.REGULAR((3,)), pltpu.SemaphoreType.REGULAR,
             ],

time: 283 us -> 282 us (level)
  no operation moved by 1% of the time
where the time goes in v8:
time: 282 us
  Pallas kernels  276 us (98%)
  local copies, waits for them, and re-layouts  5.89 us (2%)
    pallas_call x1, Pallas kernels, device_step(): pl.pallas_call(moe_kernel, out_shape=(jax.ShapeDtypeStruct((tok_rows, d_m...  276 us
    unnamed x1, local copies, waits for them, and re-layouts  5.89 us

profile of v8, /device:TPU:0, one launch (start us, length us, event | category | flops | bytes accessed | tf_op | source)
XLA Modules:
  0.0 281.6 jit_solution(8956079033301797005)
XLA Ops:
  0.0 275.7 %shard_map.64 = (bf16[4096,768]{1,0:T(8,128)(2,1)}, bf16[640,768]{1,0:T(8,128)(2,1)}) custom-call(bf16[4096,768]{1,0:T(8,128)(2,1)} %x_hbm.1, s32[1,4096]{1,0:T(1,128)} %bitcast.4, f32[1,4096]{1,0:T(1,128)} %bitcast.5, bf16[2,192,3072]{2,1,0:T(8,128)(2,1)} %wg_hbm.1, bf16[2,192,3072]{2,1,0:T(8,128)(2,1)} %wu_hbm.1, bf16[2,192,3072]{2,1,0:T(8,128)(2,1)} %bitcast.3), custom_call_target="tpu_custom_call" | custom-call | tf_op jit(solution)/shard_map/pallas_call | solution.py:674
  275.7 5.9 %copy.8 = bf16[4096,768]{1,0:T(8,128)(2,1)} copy(bf16[4096,768]{1,0:T(8,128)(2,1)} %get-tuple-element.6) | data formatting | bytes 12582912
